TPU v7x, 256 devices: a whole 4x4x8 slice. The times are simulated.
256 devices in a mesh: lat: 64 (over z, x, core), depth: 4 (over y).
Axes of the slice: x: 4, y: 4, z: 8, core: 2. Of those that a mesh axis runs over, the one named last changes fastest.
Arguments:
- surface: float32 [1024, 4096], P('lat'), may hold values from -6 to 6
- velocity: float32 [2, 1024, 4096], P(None, 'lat'), may hold values from -6 to 6
- block_map: int32 [1024, 4096], P('lat'), may hold values from 0 to 15
- free_flags: int32 [1024, 4096], P('lat'), may hold values 0 or 1
- block_rates: float32 [16], replicated, may hold values from 0.2 to 2
- previous_mesh: float32 [1024, 64, 4096], P('lat', 'depth'), may hold values from -6 to 6
Outputs:
- new_surface: float32 [1024, 4096], P('lat')
- mesh_field: float32 [1024, 64, 4096], P('lat', 'depth')
- column_norm: float32 [1024], P('lat')
All inputs are finite; a program needn't handle non-finite values. No bound on the sum of `free_flags` on one device may be relied on, other than what follows from the above.
Results may differ from a plain program's by a relative error of at most 0.00002.
Values sent between devices are 32-bit elements; how exact they have to be, the bound alone decides.
A program may use at most 64 MiB of HBM per device.

v0:
```python
import jax
import jax.numpy as jnp
from jax import lax
from jax.sharding import PartitionSpec as P

ITERS = 2


TIME_STEP = 0.5
RELAX_WEIGHT = 0.8


def extended_2(block, sides, width):
    for axis, dim in sides:
        count = lax.axis_size(axis)
        forward = [(i, i + 1) for i in range(count - 1)]
        backward = [(target, source) for source, target in forward]
        low = lax.ppermute(
            lax.slice_in_dim(block, block.shape[dim] - width, None, axis=dim), axis, forward
        )
        high = lax.ppermute(lax.slice_in_dim(block, 0, width, axis=dim), axis, backward)
        block = jnp.concatenate([low, block, high], axis=dim)
    return block


def padded(value, sides, width):
    edges = {}
    for axis, dim in sides:
        size, length = (lax.axis_size(axis), value.shape[dim])
        up = [(i, (i + 1) % size) for i in range(size - 1)]
        last = lax.slice_in_dim(value, length - width, length, axis=dim)
        leading = lax.slice_in_dim(value, 0, width, axis=dim)
        edges[dim] = (
            lax.ppermute(last, axis, up),
            lax.ppermute(leading, axis, [(b, a) for a, b in up]),
        )
    done = []
    for _, dim in sides:
        low, high = edges[dim]
        around = [(width, width) if d in done else (0, 0) for d in range(value.ndim)]
        value = jnp.concatenate([jnp.pad(low, around), value, jnp.pad(high, around)], axis=dim)
        done.append(dim)
    return value


def from_everyone(value, axis):
    copies = jnp.broadcast_to(value, (lax.axis_size(axis), *value.shape))
    return lax.all_to_all(copies, axis, split_axis=0, concat_axis=0, tiled=True)


def of_everyone(value, axis):
    return from_everyone(value, axis).sum(axis=0)


def advect(surface, velocity, block_map, free_flags, block_rates):
    widened = jnp.pad(surface, ((0, 0), (1, 1)))
    extended = extended_2(widened, (("lat", 0),), 1)
    middle = extended[1:-1, 1:-1]
    grad_rows = (extended[2:, 1:-1] - extended[:-2, 1:-1]) * 0.5
    grad_cols = (extended[1:-1, 2:] - extended[1:-1, :-2]) * 0.5
    laplace = (
        extended[2:, 1:-1]
        + extended[:-2, 1:-1]
        + extended[1:-1, 2:]
        + extended[1:-1, :-2]
        - 4.0 * middle
    )
    labels = jnp.arange(block_rates.shape[0], dtype=jnp.int32)
    matches = block_map[None, :, :] == labels[:, None, None]
    diffusivity = jnp.sum(jnp.where(matches, block_rates[:, None, None], 0.0), axis=0)
    velocity_rows = velocity[0]
    velocity_cols = velocity[1]
    tendency = -velocity_rows * grad_rows - velocity_cols * grad_cols + diffusivity * laplace
    return middle + TIME_STEP * free_flags.astype(jnp.float32) * tendency


def relax_core(extended):
    current = extended[1:-1, 1:-1]
    across_rows = extended[2:, 1:-1] + extended[:-2, 1:-1]
    padded_cols = jnp.pad(current, ((0, 0), (0, 0), (1, 1)))
    across_cols = padded_cols[:, :, 2:] + padded_cols[:, :, :-2]
    upper = extended[1:-1, :-2]
    lower = extended[1:-1, 2:]
    neighbours = across_rows + across_cols + upper + lower
    return (current, (1.0 - RELAX_WEIGHT) * current + RELAX_WEIGHT * neighbours / 6.0)


def per_device(surface, velocity, block_map, free_flags, block_rates, previous_mesh):
    columns = surface.shape[1]
    new_surface = advect(surface, velocity, block_map, free_flags, block_rates)
    surface_shift = new_surface - surface
    layers_here = previous_mesh.shape[1]
    total_layers = layers_here * lax.axis_size("depth")
    at_top = lax.axis_index("depth") == 0
    layers = lax.axis_index("depth") * layers_here + jnp.arange(layers_here, dtype=jnp.int32)
    profile = (total_layers - layers).astype(jnp.float32) / total_layers
    field = previous_mesh + surface_shift[:, None, :] * profile[None, :, None]
    for sweep_index in range(ITERS):
        extended = padded(field, (("lat", 0), ("depth", 1)), 1)
        ghost = jnp.where(at_top, surface_shift, extended[1:-1, 0, :])
        extended = extended.at[1:-1, 0, :].set(ghost)
        current, field = relax_core(extended)
    local_sums = jnp.sum(field * field, axis=(1, 2))
    total_sums = of_everyone(local_sums, "depth")
    column_norm = jnp.sqrt(total_sums / (total_layers * columns))
    return (new_surface, field, column_norm)


def solution(mesh):
    in_specs = (
        P("lat", None),
        P(None, "lat", None),
        P("lat", None),
        P("lat", None),
        P(),
        P("lat", "depth", None),
    )
    out_specs = (P("lat", None), P("lat", "depth", None), P("lat"))
    return jax.shard_map(
        per_device, mesh=mesh, in_specs=in_specs, out_specs=out_specs, check_vma=False
    )
```

profile of v0, /device:TPU:128, one launch (start us, length us, event | category | flops | bytes accessed | tf_op | source)
XLA Modules:
  0.0 102.5 jit_solution(8820315259140771022)
XLA Ops:
  0.6 1.1 %pad_slice_fusion.1 = (f32[1,4098]{1,0:T(1,128)S(1)}, f32[1,4098]{1,0:T(1,128)S(1)}) fusion(f32[16,4096]{1,0:T(8,128)} %param.10), kind=kLoop, calls=%fused_computation.37 | loop fusion | bytes 294928 | tf_op jit(solution)/shard_map/slice | solution.py:21
  1.7 3.7 %collective-permute-start = (f32[1,4098]{1,0:T(1,128)S(1)}, f32[1,4098]{1,0:T(1,128)S(1)}, u32[]{:S(2)}, u32[]{:S(2)}) collective-permute-start(f32[1,4098]{1,0:T(1,128)S(1)} %get-tuple-element.48), channel_id=1, source_target_pairs={{4,0},{8,4},{12,8},{16,12},{20,16},{24,20},{28,24},{32,28},{36,32}... | collective-permute-start | bytes 49184 | tf_op jit(solution)/shard_map/ppermute | solution.py:21
  5.4 1.9 %collective-permute-start.1 = (f32[1,4098]{1,0:T(1,128)S(1)}, f32[1,4098]{1,0:T(1,128)S(1)}, u32[]{:S(2)}, u32[]{:S(2)}) collective-permute-start(f32[1,4098]{1,0:T(1,128)S(1)} %get-tuple-element.49), channel_id=1, source_target_pairs={{0,4},{4,8},{8,12},{12,16},{16,20},{20,24},{24,28},{28,32},{32,36}... | collective-permute-start | bytes 49184 | tf_op jit(solution)/shard_map/ppermute | solution.py:18
  7.3 1.5 %select_reduce_fusion = f32[16,4096]{1,0:T(8,128)S(1)} fusion(f32[16]{0:T(128)} %param.14, s32[16,4096]{1,0:T(8,128)} %param.12), kind=kLoop, calls=%fused_computation.20 | loop fusion | flops 3080192 | bytes 524352 | tf_op jit(solution)/shard_map/reduce_sum | solution.py:70
  8.8 1.1 %pad.32 = f32[16,4098]{1,0:T(8,128)S(1)} pad(f32[16,4096]{1,0:T(8,128)} %param.10, f32[]{:T(128)} %constant.74.clone.1), padding=0_0x1_1 | pad | bytes 524420 | tf_op jit(solution)/shard_map/jit(_pad)/pad | solution.py:56
  9.9 3.9 %collective-permute-done.1 = f32[1,4098]{1,0:T(1,128)S(1)} collective-permute-done((f32[1,4098]{1,0:T(1,128)S(1)}, f32[1,4098]{1,0:T(1,128)S(1)}, u32[]{:S(2)}, u32[]{:S(2)}) %collective-permute-start.1) | collective-permute-done | bytes 16424 | tf_op jit(solution)/shard_map/ppermute | solution.py:18
  13.8 2.2 %fusion.13 = (f32[16,4096]{1,0:T(8,128)S(1)}, f32[16,4096]{1,0:T(8,128)}) fusion(f32[16,4096]{1,0:T(8,128)} %param.10, f32[16,4096]{1,0:T(8,128)S(1)} %select_reduce_fusion, f32[16,4098]{1,0:T(8,128)S(1)} %pad.32, f32[2,16,4096]{2,1,0:T(8,128)} %param.11, f32[1,4098]{1,0:T(1,128)S(1)} %collective-permute-done.1, f32[1,4098]{1,0:T(1,128)S(1)} %collective-permute-done, ...), kind=kLoop, calls=%fused_computation.38 | loop fusion | flops 1441792 | bytes 2663424 | tf_op jit(solution)/shard_map/sub | solution.py:91
  16.0 4.6 %copy_add_fusion = f32[16,16,4096]{2,0,1:T(8,128)S(1)} fusion(f32[16,16,4096]{2,1,0:T(8,128)} %param.15, f32[16]{0:T(128)S(1)} %convert_multiply_fusion, f32[16,4096]{1,0:T(8,128)S(1)} %get-tuple-element.38), kind=kLoop, calls=%fused_computation.18 | loop fusion | flops 2097152 | bytes 8650816 | tf_op jit(solution)/shard_map/add | solution.py:97
  20.7 3.5 %collective-permute-start.2 = (f32[16,1,4096]{2,0,1:T(8,128)S(1)}, f32[16,1,4096]{2,0,1:T(8,128)S(1)}, u32[]{:S(2)}, u32[]{:S(2)}) collective-permute-start(f32[16,1,4096]{2,0,1:T(8,128)S(1)} %get-tuple-element.46), channel_id=1, source_target_pairs={{0,1},{1,2},{2,3},{4,5},{5,6},{6,7},{8,9},{9,10},{10,11},{12,13},{... | collective-permute-start | bytes 786440 | tf_op jit(solution)/shard_map/ppermute | solution.py:34
  24.6 1.9 %collective-permute-start.3 = (f32[1,16,4096]{2,0,1:T(1,128)S(1)}, f32[1,16,4096]{2,0,1:T(1,128)S(1)}, u32[]{:S(2)}, u32[]{:S(2)}) collective-permute-start(f32[1,16,4096]{2,0,1:T(1,128)S(1)} %get-tuple-element.44), channel_id=1, source_target_pairs={{0,4},{4,8},{8,12},{12,16},{16,20},{20,24},{24,28},{28,32},{32,36}... | collective-permute-start | bytes 786440 | tf_op jit(solution)/shard_map/ppermute | solution.py:34
  26.6 7.0 %collective-permute-start.4 = (f32[1,16,4096]{2,0,1:T(1,128)S(1)}, f32[1,16,4096]{2,0,1:T(1,128)S(1)}, u32[]{:S(2)}, u32[]{:S(2)}) collective-permute-start(f32[1,16,4096]{2,0,1:T(1,128)S(1)} %get-tuple-element.45), channel_id=1, source_target_pairs={{4,0},{8,4},{12,8},{16,12},{20,16},{24,20},{28,24},{32,28},{36,32}... | collective-permute-start | bytes 786440 | tf_op jit(solution)/shard_map/ppermute | solution.py:35
  33.5 1.3 %collective-permute-start.5 = (f32[16,1,4096]{2,0,1:T(8,128)S(1)}, f32[16,1,4096]{2,0,1:T(8,128)S(1)}, u32[]{:S(2)}, u32[]{:S(2)}) collective-permute-start(f32[16,1,4096]{2,0,1:T(8,128)S(1)} %get-tuple-element.47), channel_id=1, source_target_pairs={{1,0},{2,1},{3,2},{5,4},{6,5},{7,6},{9,8},{10,9},{11,10},{13,12},{... | collective-permute-start | bytes 786440 | tf_op jit(solution)/shard_map/ppermute | solution.py:35
  35.6 1.8 %collective-permute-done.4 = f32[1,16,4096]{2,0,1:T(1,128)S(1)} collective-permute-done((f32[1,16,4096]{2,0,1:T(1,128)S(1)}, f32[1,16,4096]{2,0,1:T(1,128)S(1)}, u32[]{:S(2)}, u32[]{:S(2)}) %collective-permute-start.4) | collective-permute-done | bytes 262176 | tf_op jit(solution)/shard_map/ppermute | solution.py:35
  37.4 4.4 %collective-permute-done.5 = f32[16,1,4096]{2,0,1:T(8,128)S(1)} collective-permute-done((f32[16,1,4096]{2,0,1:T(8,128)S(1)}, f32[16,1,4096]{2,0,1:T(8,128)S(1)}, u32[]{:S(2)}, u32[]{:S(2)}) %collective-permute-start.5) | collective-permute-done | bytes 262176 | tf_op jit(solution)/shard_map/ppermute | solution.py:35
  41.8 3.6 %select_maximum_fusion.2 = f32[18,18,4096]{2,0,1:T(8,128)} fusion(f32[16,1,4096]{2,0,1:T(8,128)S(1)} %collective-permute-done.5, f32[16,1,4096]{2,0,1:T(8,128)S(1)} %collective-permute-done.2, f32[1,16,4096]{2,0,1:T(1,128)S(1)} %collective-permute-done.4, f32[16,16,4096]{2,0,1:T(8,128)S(1)} %copy_add_fusion, f32[1,16,4096]{2,0,1:T(1,128)S(1)} %collective-permute-done.3), kind=kLoop, calls=%fused_computation.2 | loop fusion | flops 10616832 | bytes 10551296 | tf_op jit(solution)/shard_map/concatenate | solution.py:41
  45.4 1.7 %scatter.6 = f32[18,18,4096]{2,0,1:T(8,128)} dynamic-update-slice(f32[18,18,4096]{2,0,1:T(8,128)} %select_maximum_fusion.2, f32[16,1,4096]{2,0,1:T(8,128)S(1)} %fusion.7, s32[]{:T(128)} %constant.81.clone.1, s32[]{:T(128)} %constant.80.clone.1, s32[]{:T(128)} %constant.80.clone.1) | dynamic-update-slice | bytes 524292 | tf_op jit(solution)/shard_map/scatter | solution.py:101
  47.1 3.6 %slice.183 = f32[16,16,4096]{2,0,1:T(8,128)S(1)} slice(f32[18,18,4096]{2,0,1:T(8,128)} %scatter.6), slice={[1:17], [1:17], [0:4096]} | slice | bytes 8388608 | tf_op jit(solution)/shard_map/slice | solution.py:78
  50.8 1.2 %copy-done = f32[18,18,4096]{2,0,1:T(8,128)S(1)} copy-done((f32[18,18,4096]{2,0,1:T(8,128)S(1)}, f32[18,18,4096]{2,0,1:T(8,128)}, u32[]{:S(2)}) %copy-start) | copy-done | bytes 5308440
  52.0 3.2 %fusion.4 = f32[16,16,4096]{2,0,1:T(8,128)S(1)} fusion(f32[18,18,4096]{2,0,1:T(8,128)S(1)} %copy-done, f32[16,16,4096]{2,0,1:T(8,128)S(1)} %slice.183), kind=kLoop, calls=%fused_computation.14 | loop fusion | flops 8388608 | bytes 25165824 | tf_op jit(solution)/shard_map/add | solution.py:85
  55.2 3.5 %collective-permute-start.6 = (f32[16,1,4096]{2,0,1:T(8,128)S(1)}, f32[16,1,4096]{2,0,1:T(8,128)S(1)}, u32[]{:S(2)}, u32[]{:S(2)}) collective-permute-start(f32[16,1,4096]{2,0,1:T(8,128)S(1)} %get-tuple-element.42), channel_id=1, source_target_pairs={{0,1},{1,2},{2,3},{4,5},{5,6},{6,7},{8,9},{9,10},{10,11},{12,13},{... | collective-permute-start | bytes 786440 | tf_op jit(solution)/shard_map/ppermute | solution.py:34
  59.1 1.9 %collective-permute-start.7 = (f32[1,16,4096]{2,0,1:T(1,128)S(1)}, f32[1,16,4096]{2,0,1:T(1,128)S(1)}, u32[]{:S(2)}, u32[]{:S(2)}) collective-permute-start(f32[1,16,4096]{2,0,1:T(1,128)S(1)} %get-tuple-element.40), channel_id=1, source_target_pairs={{0,4},{4,8},{8,12},{12,16},{16,20},{20,24},{24,28},{28,32},{32,36}... | collective-permute-start | bytes 786440 | tf_op jit(solution)/shard_map/ppermute | solution.py:34
  61.0 7.0 %collective-permute-start.8 = (f32[1,16,4096]{2,0,1:T(1,128)S(1)}, f32[1,16,4096]{2,0,1:T(1,128)S(1)}, u32[]{:S(2)}, u32[]{:S(2)}) collective-permute-start(f32[1,16,4096]{2,0,1:T(1,128)S(1)} %get-tuple-element.41), channel_id=1, source_target_pairs={{4,0},{8,4},{12,8},{16,12},{20,16},{24,20},{28,24},{32,28},{36,32}... | collective-permute-start | bytes 786440 | tf_op jit(solution)/shard_map/ppermute | solution.py:35
  68.0 1.3 %collective-permute-start.9 = (f32[16,1,4096]{2,0,1:T(8,128)S(1)}, f32[16,1,4096]{2,0,1:T(8,128)S(1)}, u32[]{:S(2)}, u32[]{:S(2)}) collective-permute-start(f32[16,1,4096]{2,0,1:T(8,128)S(1)} %get-tuple-element.43), channel_id=1, source_target_pairs={{1,0},{2,1},{3,2},{5,4},{6,5},{7,6},{9,8},{10,9},{11,10},{13,12},{... | collective-permute-start | bytes 786440 | tf_op jit(solution)/shard_map/ppermute | solution.py:35
  70.1 1.8 %collective-permute-done.8 = f32[1,16,4096]{2,0,1:T(1,128)S(1)} collective-permute-done((f32[1,16,4096]{2,0,1:T(1,128)S(1)}, f32[1,16,4096]{2,0,1:T(1,128)S(1)}, u32[]{:S(2)}, u32[]{:S(2)}) %collective-permute-start.8) | collective-permute-done | bytes 262176 | tf_op jit(solution)/shard_map/ppermute | solution.py:35
  71.9 4.4 %collective-permute-done.9 = f32[16,1,4096]{2,0,1:T(8,128)S(1)} collective-permute-done((f32[16,1,4096]{2,0,1:T(8,128)S(1)}, f32[16,1,4096]{2,0,1:T(8,128)S(1)}, u32[]{:S(2)}, u32[]{:S(2)}) %collective-permute-start.9) | collective-permute-done | bytes 262176 | tf_op jit(solution)/shard_map/ppermute | solution.py:35
  76.3 3.5 %select_maximum_fusion = f32[18,18,4096]{2,0,1:T(8,128)} fusion(f32[16,1,4096]{2,0,1:T(8,128)S(1)} %collective-permute-done.9, f32[16,1,4096]{2,0,1:T(8,128)S(1)} %collective-permute-done.6, f32[1,16,4096]{2,0,1:T(1,128)S(1)} %collective-permute-done.8, f32[16,16,4096]{2,0,1:T(8,128)S(1)} %fusion.4, f32[1,16,4096]{2,0,1:T(1,128)S(1)} %collective-permute-done.7), kind=kLoop, calls=%fused_computation | loop fusion | flops 10616832 | bytes 10551296 | tf_op jit(solution)/shard_map/concatenate | solution.py:41
  79.8 1.7 %scatter.9 = f32[18,18,4096]{2,0,1:T(8,128)} dynamic-update-slice(f32[18,18,4096]{2,0,1:T(8,128)} %select_maximum_fusion, f32[16,1,4096]{2,0,1:T(8,128)S(1)} %fusion.6, s32[]{:T(128)} %constant.81.clone.1, s32[]{:T(128)} %constant.80.clone.1, s32[]{:T(128)} %constant.80.clone.1) | dynamic-update-slice | bytes 524292 | tf_op jit(solution)/shard_map/scatter | solution.py:101
  81.5 3.6 %slice.192 = f32[16,16,4096]{2,0,1:T(8,128)S(1)} slice(f32[18,18,4096]{2,0,1:T(8,128)} %scatter.9), slice={[1:17], [1:17], [0:4096]} | slice | bytes 8388608 | tf_op jit(solution)/shard_map/slice | solution.py:78
  85.2 1.2 %copy-done.1 = f32[18,18,4096]{2,0,1:T(8,128)S(1)} copy-done((f32[18,18,4096]{2,0,1:T(8,128)S(1)}, f32[18,18,4096]{2,0,1:T(8,128)}, u32[]{:S(2)}) %copy-start.1) | copy-done | bytes 5308440
  86.3 4.9 %multiply_reduce_fusion = (f32[16]{0:T(128)S(1)}, f32[16,16,4096]{2,0,1:T(8,128)}) fusion(f32[18,18,4096]{2,0,1:T(8,128)S(1)} %copy-done.1, f32[16,16,4096]{2,0,1:T(8,128)S(1)} %slice.192), kind=kLoop, calls=%fused_computation.19 | loop fusion | flops 10485744 | bytes 25165888 | tf_op jit(solution)/shard_map/reduce_sum | solution.py:103
  91.9 3.4 %all-to-all-start = ((f32[4,1,16]{2,1,0:T(1,128)}), f32[4,1,16]{2,1,0:T(1,128)S(1)}, u32[]{:S(2)}, u32[]{:S(2)}) async-start(f32[4,1,16]{2,1,0:T(1,128)} %broadcast_in_dim.22), calls=%async_computation | async-start | bytes 4096 | tf_op jit(solution)/shard_map/all_to_all | solution.py:48
  95.3 6.6 %copy.20 = f32[16,16,4096]{2,1,0:T(8,128)} copy(f32[16,16,4096]{2,0,1:T(8,128)} %get-tuple-element.37) | data formatting | bytes 8388608
  (18 shorter events, 3.7 us)
Async XLA Ops:
  1.7 8.2 %collective-permute-start = (f32[1,4098]{1,0:T(1,128)S(1)}, f32[1,4098]{1,0:T(1,128)S(1)}, u32[]{:S(2)}, u32[]{:S(2)}) collective-permute-start(f32[1,4098]{1,0:T(1,128)S(1)} %get-tuple-element.48), channel_id=1, source_target_pairs={{4,0},{8,4},{12,8},{16,12},{20,16},{24,20},{28,24},{32,28},{36,32}... | collective-permute-start | bytes 49184 | tf_op jit(solution)/shard_map/ppermute | solution.py:21
  5.4 8.4 %collective-permute-start.1 = (f32[1,4098]{1,0:T(1,128)S(1)}, f32[1,4098]{1,0:T(1,128)S(1)}, u32[]{:S(2)}, u32[]{:S(2)}) collective-permute-start(f32[1,4098]{1,0:T(1,128)S(1)} %get-tuple-element.49), channel_id=1, source_target_pairs={{0,4},{4,8},{8,12},{12,16},{16,20},{20,24},{24,28},{28,32},{32,36}... | collective-permute-start | bytes 49184 | tf_op jit(solution)/shard_map/ppermute | solution.py:18
  20.7 14.1 %collective-permute-start.2 = (f32[16,1,4096]{2,0,1:T(8,128)S(1)}, f32[16,1,4096]{2,0,1:T(8,128)S(1)}, u32[]{:S(2)}, u32[]{:S(2)}) collective-permute-start(f32[16,1,4096]{2,0,1:T(8,128)S(1)} %get-tuple-element.46), channel_id=1, source_target_pairs={{0,1},{1,2},{2,3},{4,5},{5,6},{6,7},{8,9},{9,10},{10,11},{12,13},{... | collective-permute-start | bytes 786440 | tf_op jit(solution)/shard_map/ppermute | solution.py:34
  24.6 11.0 %collective-permute-start.3 = (f32[1,16,4096]{2,0,1:T(1,128)S(1)}, f32[1,16,4096]{2,0,1:T(1,128)S(1)}, u32[]{:S(2)}, u32[]{:S(2)}) collective-permute-start(f32[1,16,4096]{2,0,1:T(1,128)S(1)} %get-tuple-element.44), channel_id=1, source_target_pairs={{0,4},{4,8},{8,12},{12,16},{16,20},{20,24},{24,28},{28,32},{32,36}... | collective-permute-start | bytes 786440 | tf_op jit(solution)/shard_map/ppermute | solution.py:34
  26.6 10.8 %collective-permute-start.4 = (f32[1,16,4096]{2,0,1:T(1,128)S(1)}, f32[1,16,4096]{2,0,1:T(1,128)S(1)}, u32[]{:S(2)}, u32[]{:S(2)}) collective-permute-start(f32[1,16,4096]{2,0,1:T(1,128)S(1)} %get-tuple-element.45), channel_id=1, source_target_pairs={{4,0},{8,4},{12,8},{16,12},{20,16},{24,20},{28,24},{32,28},{36,32}... | collective-permute-start | bytes 786440 | tf_op jit(solution)/shard_map/ppermute | solution.py:35
  33.5 8.3 %collective-permute-start.5 = (f32[16,1,4096]{2,0,1:T(8,128)S(1)}, f32[16,1,4096]{2,0,1:T(8,128)S(1)}, u32[]{:S(2)}, u32[]{:S(2)}) collective-permute-start(f32[16,1,4096]{2,0,1:T(8,128)S(1)} %get-tuple-element.47), channel_id=1, source_target_pairs={{1,0},{2,1},{3,2},{5,4},{6,5},{7,6},{9,8},{10,9},{11,10},{13,12},{... | collective-permute-start | bytes 786440 | tf_op jit(solution)/shard_map/ppermute | solution.py:35
  47.1 4.8 %copy-start = (f32[18,18,4096]{2,0,1:T(8,128)S(1)}, f32[18,18,4096]{2,0,1:T(8,128)}, u32[]{:S(2)}) copy-start(f32[18,18,4096]{2,0,1:T(8,128)} %scatter.6) | copy-start | bytes 15925252
  55.2 14.1 %collective-permute-start.6 = (f32[16,1,4096]{2,0,1:T(8,128)S(1)}, f32[16,1,4096]{2,0,1:T(8,128)S(1)}, u32[]{:S(2)}, u32[]{:S(2)}) collective-permute-start(f32[16,1,4096]{2,0,1:T(8,128)S(1)} %get-tuple-element.42), channel_id=1, source_target_pairs={{0,1},{1,2},{2,3},{4,5},{5,6},{6,7},{8,9},{9,10},{10,11},{12,13},{... | collective-permute-start | bytes 786440 | tf_op jit(solution)/shard_map/ppermute | solution.py:34
  59.1 11.0 %collective-permute-start.7 = (f32[1,16,4096]{2,0,1:T(1,128)S(1)}, f32[1,16,4096]{2,0,1:T(1,128)S(1)}, u32[]{:S(2)}, u32[]{:S(2)}) collective-permute-start(f32[1,16,4096]{2,0,1:T(1,128)S(1)} %get-tuple-element.40), channel_id=1, source_target_pairs={{0,4},{4,8},{8,12},{12,16},{16,20},{20,24},{24,28},{28,32},{32,36}... | collective-permute-start | bytes 786440 | tf_op jit(solution)/shard_map/ppermute | solution.py:34
  61.0 10.8 %collective-permute-start.8 = (f32[1,16,4096]{2,0,1:T(1,128)S(1)}, f32[1,16,4096]{2,0,1:T(1,128)S(1)}, u32[]{:S(2)}, u32[]{:S(2)}) collective-permute-start(f32[1,16,4096]{2,0,1:T(1,128)S(1)} %get-tuple-element.41), channel_id=1, source_target_pairs={{4,0},{8,4},{12,8},{16,12},{20,16},{24,20},{28,24},{32,28},{36,32}... | collective-permute-start | bytes 786440 | tf_op jit(solution)/shard_map/ppermute | solution.py:35
  68.0 8.3 %collective-permute-start.9 = (f32[16,1,4096]{2,0,1:T(8,128)S(1)}, f32[16,1,4096]{2,0,1:T(8,128)S(1)}, u32[]{:S(2)}, u32[]{:S(2)}) collective-permute-start(f32[16,1,4096]{2,0,1:T(8,128)S(1)} %get-tuple-element.43), channel_id=1, source_target_pairs={{1,0},{2,1},{3,2},{5,4},{6,5},{7,6},{9,8},{10,9},{11,10},{13,12},{... | collective-permute-start | bytes 786440 | tf_op jit(solution)/shard_map/ppermute | solution.py:35
  81.5 4.8 %copy-start.1 = (f32[18,18,4096]{2,0,1:T(8,128)S(1)}, f32[18,18,4096]{2,0,1:T(8,128)}, u32[]{:S(2)}) copy-start(f32[18,18,4096]{2,0,1:T(8,128)} %scatter.9) | copy-start | bytes 15925252
  91.9 10.1 %all-to-all-start = ((f32[4,1,16]{2,1,0:T(1,128)}), f32[4,1,16]{2,1,0:T(1,128)S(1)}, u32[]{:S(2)}, u32[]{:S(2)}) async-start(f32[4,1,16]{2,1,0:T(1,128)} %broadcast_in_dim.22), calls=%async_computation | async-start | bytes 4096 | tf_op jit(solution)/shard_map/all_to_all | solution.py:48
where the time goes:
time: 103 us; the launch traced here: 102 us
  starting transfers between devices  36.3 us (35%)
  other arithmetic  24.2 us (23%)
  local copies, waits for them, and re-layouts  23.4 us (23%)
  waiting for transfers between devices  17.7 us (17%)
    ppermute x4, starting transfers between devices, padded(): lax.ppermute(leading, axis, [(b, a) for a, b in up])  16.5 us
    ppermute x4, waiting for transfers between devices, padded(): lax.ppermute(leading, axis, [(b, a) for a, b in up])  12.3 us
    ppermute x4, starting transfers between devices, padded(): lax.ppermute(last, axis, up)  10.8 us
    unnamed x5, local copies, waits for them, and re-layouts  9.01 us
    slice x2, local copies, waits for them, and re-layouts, relax_core(): current = extended[1:-1, 1:-1]  7.25 us
    concatenate x2, other arithmetic, padded(): jnp.concatenate([jnp.pad(low, around), value, jnp.pad(high, around)], axi...  7.11 us
    reduce_sum x1, other arithmetic, per_device(): local_sums = jnp.sum(field * field, axis=(1, 2))  4.94 us
    add x1, other arithmetic, per_device(): field = previous_mesh + surface_shift[:, None, :] * profile[None, :, None]  4.64 us
  transfers between devices with their start and end apart: 11, of which 7 were waited for; matrix products, arithmetic and copies ran while one was open for 10% of the time, Pallas kernels for 0%

commit v1 on v0

v1 whole, which is shorter than its diff:
```python
import jax
import jax.numpy as jnp
from jax import lax
from jax.experimental import pallas as pl
from jax.experimental.pallas import tpu as pltpu
from jax.sharding import PartitionSpec as P

MESH = pl.DeviceIdType.MESH
TIME_STEP = 0.5
RELAX_WEIGHT = 0.8
KEEP = 1.0 - RELAX_WEIGHT
SHARE = RELAX_WEIGHT / 6.0
CENTRE = KEEP / SHARE
SCALE = SHARE * SHARE
SUB = 8
CHUNKS = 8


def iotas(width):
    lane = lax.broadcasted_iota(jnp.int32, (SUB, 128), 1)
    sub = lax.broadcasted_iota(jnp.int32, (SUB, 128), 0)
    return lane, sub


def before(v, masks):
    width = v.shape[-1]
    rolled = pltpu.roll(v, 1, 1)
    first = rolled[:, :128]
    carried = pltpu.roll(first, 1, 0)
    first = jnp.where(masks[0], jnp.where(masks[1], 0.0, carried), first)
    return jnp.concatenate([first, rolled[:, 128:]], axis=1)


def after(v, masks):
    width = v.shape[-1]
    rolled = pltpu.roll(v, width - 1, 1)
    last = rolled[:, width - 128:]
    carried = pltpu.roll(last, SUB - 1, 0)
    last = jnp.where(masks[2], jnp.where(masks[3], 0.0, carried), last)
    return jnp.concatenate([rolled[:, : width - 128], last], axis=1)


def relax_kernel(
    rows, layers, width, n_lat, n_depth,
    surface, velocity, block_map, free_flags, block_rates, previous,
    new_surface, mesh_out, norm_out,
    prev, once, above, below, surf, vel, bmap, flags, rates,
    shift, wide, widest, squares, totals,
    load_sem, up_send, up_recv, down_send, down_recv, side_send, side_recv,
    corner_send, corner_recv, sum_send, sum_recv,
):
    lat = lax.axis_index("lat")
    depth = lax.axis_index("depth")
    has_left, has_right = lat > 0, lat < n_lat - 1
    has_up, has_down = depth > 0, depth < n_depth - 1
    left, right = {"lat": lat - 1}, {"lat": lat + 1}
    up, down = {"depth": depth - 1}, {"depth": depth + 1}

    barrier = pltpu.get_barrier_semaphore()
    for k in (1, n_depth - 1):
        pl.semaphore_signal(
            barrier, inc=1, device_id={"depth": lax.rem(depth + k, n_depth)}, device_id_type=MESH)
    for have, target in ((has_left, left), (has_right, right)):
        @pl.when(have)
        def _():
            pl.semaphore_signal(barrier, inc=1, device_id=target, device_id_type=MESH)

    count = 0
    groups = {}

    def load(name, pairs):
        nonlocal count
        copies = []
        for src, dst in pairs:
            copy = pltpu.make_async_copy(src, dst, load_sem.at[count])
            copy.start()
            copies.append(copy)
            count += 1
        groups[name] = copies

    def loaded(name):
        for copy in groups[name]:
            copy.wait()

    cols = [slice(s * width, (s + 1) * width) for s in range(SUB)]
    own = slice(2, 2 + rows)
    load("outer", [
        (previous.at[:, part, cols[s]], prev.at[own, part, s, :])
        for part in (slice(layers - 2, layers), slice(0, 2)) for s in range(SUB)
    ])
    load("surface",
         [(surface.at[:, cols[s]], surf.at[slice(3, 3 + rows), s, :]) for s in range(SUB)]
         + [(velocity.at[:, :, cols[s]], vel.at[:, own, s, :]) for s in range(SUB)]
         + [(block_map.at[:, cols[s]], bmap.at[own, s, :]) for s in range(SUB)]
         + [(free_flags.at[:, cols[s]], flags.at[own, s, :]) for s in range(SUB)]
         + [(block_rates, rates)])
    load("inner", [
        (previous.at[:, part, cols[s]], prev.at[own, part, s, :])
        for part in (slice(2, SUB), slice(layers - SUB, layers - 2)) for s in range(SUB)
    ])

    def clear(ref):
        ref[...] = jnp.zeros(ref.shape, ref.dtype)

    @pl.when(jnp.logical_not(has_up))
    def _():
        clear(above)

    @pl.when(jnp.logical_not(has_down))
    def _():
        clear(below)

    for have, near, far, at in (
        (has_left, slice(0, 2), slice(0, 3), 0),
        (has_right, slice(rows + 2, rows + 4), slice(rows + 3, rows + 6), rows + 1),
    ):
        @pl.when(jnp.logical_not(have))
        def _():
            clear(prev.at[near])
            clear(surf.at[far])
            clear(vel.at[:, near])
            clear(bmap.at[near])
            clear(flags.at[near])
            clear(above.at[at])
            clear(below.at[at])
            clear(once.at[at])

    pl.semaphore_wait(barrier, 2 + has_left.astype(jnp.int32) + has_right.astype(jnp.int32))

    def remote(src, dst, send, recv, target):
        return pltpu.make_async_remote_copy(
            src_ref=src, dst_ref=dst, send_sem=send, recv_sem=recv,
            device_id=target, device_id_type=MESH,
        )

    step = rows // CHUNKS
    last_two, first_two = slice(layers - 2, layers), slice(0, 2)
    to_down, to_up = [], []
    for c in range(CHUNKS):
        mine = slice(2 + c * step, 2 + (c + 1) * step)
        theirs = slice(1 + c * step, 1 + (c + 1) * step)
        to_down.append(remote(prev.at[mine, last_two], above.at[theirs], down_send.at[c], down_recv.at[c], down))
        to_up.append(remote(prev.at[mine, first_two], below.at[theirs], up_send.at[c], up_recv.at[c], up))

    loaded("outer")

    @pl.when(has_down)
    def _():
        for copy in to_down:
            copy.start()

    @pl.when(has_up)
    def _():
        for copy in to_up:
            copy.start()

    def sides(mine3, theirs3, mine2, theirs2, row, target):
        return [
            remote(surf.at[mine3], surf.at[theirs3], side_send.at[row, 0], side_recv.at[row, 0], target),
            remote(vel.at[:, mine2], vel.at[:, theirs2], side_send.at[row, 1], side_recv.at[row, 1], target),
            remote(bmap.at[mine2], bmap.at[theirs2], side_send.at[row, 2], side_recv.at[row, 2], target),
            remote(flags.at[mine2], flags.at[theirs2], side_send.at[row, 3], side_recv.at[row, 3], target),
            remote(prev.at[mine2], prev.at[theirs2], side_send.at[row, 4], side_recv.at[row, 4], target),
        ]

    to_right = sides(slice(rows, rows + 3), slice(0, 3), slice(rows, rows + 2), slice(0, 2), 0, right)
    to_left = sides(slice(3, 6), slice(rows + 3, rows + 6), slice(2, 4), slice(rows + 2, rows + 4), 1, left)

    loaded("surface")

    @pl.when(has_right)
    def _():
        for copy in to_right[:4]:
            copy.start()

    @pl.when(has_left)
    def _():
        for copy in to_left[:4]:
            copy.start()

    loaded("inner")

    @pl.when(has_right)
    def _():
        to_right[4].start()

    @pl.when(has_left)
    def _():
        to_left[4].start()

    lane, sub = iotas(width)
    masks = (lane == 0, sub == 0, lane == 127, sub == SUB - 1)

    def neighbours(v):
        return before(v, masks) + after(v, masks)

    def sweep_once(i, carry):
        here = prev[i + 1, 0]
        earlier = None
        for z in range(layers):
            later = prev[i + 1, z + 1] if z < layers - 1 else None
            total = CENTRE * here + (prev[i, z] + prev[i + 2, z]) + neighbours(here)
            if earlier is not None:
                total = total + earlier
            if later is not None:
                total = total + later
            once[i, z] = total
            earlier, here = here, later
        return carry

    lax.fori_loop(2, rows, sweep_once, 0)

    @pl.when(has_left)
    def _():
        for copy in to_right[:4]:
            copy.wait_recv()

    @pl.when(has_right)
    def _():
        for copy in to_left[:4]:
            copy.wait_recv()

    corners = []
    for number, (src, dst, lat_to, depth_to, have_to, lat_from, depth_from) in enumerate((
        (prev.at[rows + 1, layers - 1], above.at[0, 1], lat + 1, depth + 1, (has_right, has_down), has_left, has_up),
        (prev.at[2, layers - 1], above.at[rows + 1, 1], lat - 1, depth + 1, (has_left, has_down), has_right, has_up),
        (prev.at[rows + 1, 0], below.at[0, 0], lat + 1, depth - 1, (has_right, has_up), has_left, has_down),
        (prev.at[2, 0], below.at[rows + 1, 0], lat - 1, depth - 1, (has_left, has_up), has_right, has_down),
    )):
        copy = remote(src, dst, corner_send.at[number], corner_recv.at[number], {"lat": lat_to, "depth": depth_to})
        goes = jnp.logical_and(*have_to)
        comes = jnp.logical_and(lat_from, depth_from)
        corners.append((copy, goes, comes))

        @pl.when(goes)
        def _():
            copy.start()

    rate = [rates[k] for k in range(16)]

    def lookup(index):
        level = rate
        for bit in range(4):
            odd = (index & (1 << bit)) != 0
            level = [jnp.where(odd, level[2 * k + 1], level[2 * k]) for k in range(len(level) // 2)]
        return level[0]

    def advect(i, store):
        low, middle, high = surf[i], surf[i + 1], surf[i + 2]
        west, east = before(middle, masks), after(middle, masks)
        grad_rows = (high - low) * 0.5
        grad_cols = (east - west) * 0.5
        laplace = high + low + east + west - 4.0 * middle
        tendency = -vel[0, i] * grad_rows - vel[1, i] * grad_cols + lookup(bmap[i]) * laplace
        new = middle + TIME_STEP * flags[i].astype(jnp.float32) * tendency
        if store:
            new_surface[i - 2] = new
        shift[i] = new - middle

    def advect_inner(i, carry):
        advect(i, True)
        return carry

    lax.fori_loop(2, rows + 2, advect_inner, 0)
    for i in (0, 1, rows + 2, rows + 3):
        advect(i, False)

    def widen(src, dst, i):
        here = src[i + 1]
        dst[i] = (CENTRE + 2.0) * here + (src[i] + src[i + 2]) + neighbours(here)

    def widen_once(i, carry):
        widen(shift, wide, i)
        return carry

    def widen_twice(i, carry):
        widen(wide, widest, i)
        return carry

    lax.fori_loop(0, rows + 2, widen_once, 0)

    @pl.when(jnp.logical_not(has_left))
    def _():
        clear(wide.at[0])

    @pl.when(jnp.logical_not(has_right))
    def _():
        clear(wide.at[rows + 1])

    lax.fori_loop(0, rows, widen_twice, 0)

    all_layers = layers * n_depth
    profile = [
        (all_layers - (depth * layers + z)).astype(jnp.float32) / all_layers * SCALE for z in range(layers)
    ]
    zero = jnp.float32(0.0)
    top = jnp.where(has_up, zero, jnp.float32(SCALE))
    upper = jnp.where(has_up, jnp.float32(SCALE), zero)
    lower = jnp.where(has_down, jnp.float32(SCALE), zero)

    def narrow(v):
        return sum(v[:, k * 128:(k + 1) * 128] for k in range(width // 128))

    def sweep_twice(i, carry):
        here = once[i + 1, 0]
        earlier = None
        part = widest[i]
        acc = None
        for z in range(layers):
            later = once[i + 1, z + 1] if z < layers - 1 else None
            total = CENTRE * here + (once[i, z] + once[i + 2, z]) + neighbours(here)
            if earlier is not None:
                total = total + earlier
            if later is not None:
                total = total + later
            total = SCALE * total + profile[z] * part
            if z == 0:
                total = total + upper * prev[i + 2, 0] + top * (
                    (1.0 / SHARE + 2.0 / all_layers) * shift[i + 2]
                    - (1.0 + 2.0 / all_layers) * wide[i + 1])
            elif z == 1:
                total = total - (top * (1.0 / all_layers)) * shift[i + 2]
            elif z == layers - 1:
                total = total + lower * prev[i + 2, layers - 1]
            elif z < layers - 2:
                acc = total * total if acc is None else acc + total * total
            mesh_out[i, z] = total
            earlier, here = here, later
        squares[i] = narrow(acc)
        return carry

    lax.fori_loop(2, rows - 2, sweep_twice, 0)

    @pl.when(has_left)
    def _():
        to_right[4].wait_recv()
        sweep_once(0, 0)

    @pl.when(has_right)
    def _():
        to_left[4].wait_recv()
        sweep_once(rows + 1, 0)

    sweep_once(1, 0)
    sweep_once(rows, 0)

    def at_edges(k, carry):
        sweep_twice(k, 0)
        sweep_twice(rows - 1 - k, 0)
        return carry

    lax.fori_loop(0, 2, at_edges, 0)

    def finish(i, carry):
        acc = None
        for ref, near, far, outer, inner in ((above, 1, 0, 0, 1), (below, 0, 1, layers - 1, layers - 2)):
            here = ref[i + 1, near]
            around = ref[i, near] + ref[i + 2, near] + neighbours(here)
            edge = mesh_out[i, outer] + SCALE * (2.0 * CENTRE * here + 2.0 * around + ref[i + 1, far])
            next_in = mesh_out[i, inner] + SCALE * here
            mesh_out[i, outer] = edge
            mesh_out[i, inner] = next_in
            both = edge * edge + next_in * next_in
            acc = both if acc is None else acc + both
        squares[i] = squares[i] + narrow(acc)
        return carry

    for copy, goes, comes in corners:
        @pl.when(comes)
        def _():
            copy.wait_recv()

    done = 0
    for c in range(CHUNKS):
        @pl.when(has_up)
        def _():
            to_down[c].wait_recv()

        @pl.when(has_down)
        def _():
            to_up[c].wait_recv()

        ready = rows if c == CHUNKS - 1 else (c + 1) * step - 1
        lax.fori_loop(done, ready, finish, 0)
        done = ready

    totals[depth] = jnp.sum(squares[...], axis=1)
    spread = []
    for k in range(1, n_depth):
        target = lax.rem(depth + k, n_depth)
        copy = remote(totals.at[depth], totals.at[depth], sum_send.at[k - 1], sum_recv.at[k - 1], {"depth": target})
        copy.start()
        spread.append(copy)
    for copy in spread:
        copy.wait_recv()
    total = totals[0]
    for k in range(1, n_depth):
        total = total + totals[k]
    norm = jnp.sqrt(jnp.sum(total, axis=1, keepdims=True) / (all_layers * SUB * width))
    spot = lax.broadcasted_iota(jnp.int32, (rows, 128), 0) == lax.broadcasted_iota(jnp.int32, (rows, 128), 1)
    norm_out[...] = jnp.sum(jnp.where(spot, norm, 0.0), axis=0, keepdims=True)

    @pl.when(has_down)
    def _():
        for copy in to_down:
            copy.wait_send()

    @pl.when(has_up)
    def _():
        for copy in to_up:
            copy.wait_send()

    @pl.when(has_right)
    def _():
        for copy in to_right:
            copy.wait_send()

    @pl.when(has_left)
    def _():
        for copy in to_left:
            copy.wait_send()

    for copy, goes, comes in corners:
        @pl.when(goes)
        def _():
            copy.wait_send()

    for copy in spread:
        copy.wait_send()


def store_kernel(rows, width, mesh_in, surface_in, norm_in, mesh_out, surface_out, norm_out, sem):
    copies = []
    for s in range(SUB):
        cols = slice(s * width, (s + 1) * width)
        copies.append(pltpu.make_async_copy(mesh_in.at[:, :, s, :], mesh_out.at[:, :, cols], sem.at[s]))
        copies.append(pltpu.make_async_copy(surface_in.at[:, s, :], surface_out.at[:, cols], sem.at[SUB + s]))
    for copy in copies:
        copy.start()
    norm_out[...] = norm_in[0, :rows]
    for copy in copies:
        copy.wait()


def solution(mesh):
    n_lat, n_depth = mesh.shape["lat"], mesh.shape["depth"]

    def per_device(surface, velocity, block_map, free_flags, block_rates, previous):
        rows, layers, columns = previous.shape
        width = columns // SUB
        f32 = jnp.float32

        def vmem(*shape, dtype=f32):
            return pltpu.VMEM(shape, dtype)

        def kernel(*refs):
            relax_kernel(rows, layers, width, n_lat, n_depth, *refs)

        hbm = pl.BlockSpec(memory_space=pl.ANY)
        inside = pl.BlockSpec(memory_space=pltpu.VMEM)
        dma = pltpu.SemaphoreType.DMA
        new_surface, field, norm = pl.pallas_call(
            kernel,
            out_shape=(
                jax.ShapeDtypeStruct((rows, SUB, width), f32),
                jax.ShapeDtypeStruct((rows, layers, SUB, width), f32),
                jax.ShapeDtypeStruct((1, 128), f32),
            ),
            in_specs=[hbm] * 6,
            out_specs=(inside, inside, inside),
            scratch_shapes=[
                vmem(rows + 4, layers, SUB, width),
                vmem(rows + 2, layers, SUB, width),
                vmem(rows + 2, 2, SUB, width),
                vmem(rows + 2, 2, SUB, width),
                vmem(rows + 6, SUB, width),
                vmem(2, rows + 4, SUB, width),
                vmem(rows + 4, SUB, width, dtype=jnp.int32),
                vmem(rows + 4, SUB, width, dtype=jnp.int32),
                pltpu.SMEM((16,), f32),
                vmem(rows + 4, SUB, width),
                vmem(rows + 2, SUB, width),
                vmem(rows, SUB, width),
                vmem(rows, SUB, 128),
                vmem(n_depth, rows, 128),
                dma((8 * SUB + 1,)),
                dma((CHUNKS,)), dma((CHUNKS,)), dma((CHUNKS,)), dma((CHUNKS,)),
                dma((2, 5)), dma((2, 5)),
                dma((4,)), dma((4,)),
                dma((n_depth - 1,)), dma((n_depth - 1,)),
            ],
            compiler_params=pltpu.CompilerParams(
                collective_id=0, has_side_effects=True, vmem_limit_bytes=VMEM_LIMIT
            ),
            name="relax",
        )(surface, velocity, block_map, free_flags, block_rates, previous)

        def store(*refs):
            store_kernel(rows, width, *refs)

        field, new_surface, norm = pl.pallas_call(
            store,
            out_shape=(
                jax.ShapeDtypeStruct(previous.shape, f32),
                jax.ShapeDtypeStruct(surface.shape, f32),
                jax.ShapeDtypeStruct((rows,), f32),
            ),
            in_specs=[inside, inside, inside],
            out_specs=(hbm, hbm, inside),
            scratch_shapes=[dma((2 * SUB,))],
            name="store",
        )(field, new_surface, norm)
        return new_surface, field, norm

    return jax.shard_map(
        per_device,
        mesh=mesh,
        in_specs=(
            P("lat", None), P(None, "lat", None), P("lat", None), P("lat", None), P(),
            P("lat", "depth", None),
        ),
        out_specs=(P("lat", None), P("lat", "depth", None), P("lat")),
        check_vma=False,
    )


VMEM_LIMIT = 58 * 1024 * 1024
```

time: 103 us -> 32.4 us (0.31)
  starting transfers between devices: 36.3 us -> 0 us
  Pallas kernels: 0 us -> 31.6 us
  other arithmetic: 24.2 us -> 0 us
  local copies, waits for them, and re-layouts: 23.4 us -> 0 us
  waiting for transfers between devices: 17.7 us -> 0 us
    ppermute x10 -> x0, starting transfers between devices: 32.9 us -> none  [the longest x4 16.5 us: padded(): lax.ppermute(leading, axis, [(b, a) for a, b in up])]
    pallas_call x0 -> x2, Pallas kernels: none -> 31.6 us  [the longest x1 26.6 us: per_device(): pl.pallas_call(kernel, out_shape=(jax.ShapeDtypeStruct((rows, SUB, width)...]
    ppermute x10 -> x0, waiting for transfers between devices: 17.7 us -> none  [the longest x4 12.3 us: padded(): lax.ppermute(leading, axis, [(b, a) for a, b in up])]
    slice x7 -> x0, local copies, waits for them, and re-layouts: 9.26 us -> none  [the longest x2 7.25 us: relax_core(): current = extended[1:-1, 1:-1]]
    unnamed x5 -> x0, local copies, waits for them, and re-layouts: 9.01 us -> none
    add x2 -> x0, other arithmetic: 7.8 us -> none  [the longest x1 4.64 us: per_device(): field = previous_mesh + surface_shift[:, None, :] * profile[None, :, None]]
    concatenate x2 -> x0, other arithmetic: 7.11 us -> none  [padded(): jnp.concatenate([jnp.pad(low, around), value, jnp.pad(high, around)], axi...]
    reduce_sum x3 -> x0, other arithmetic: 6.42 us -> none  [the longest x1 4.94 us: per_device(): local_sums = jnp.sum(field * field, axis=(1, 2))]
  transfers between devices with their start and end apart: 11 -> 0, of which waited for: 7 -> 0; matrix products, arithmetic and copies ran while one was open for 10% -> 0% of each run, Pallas kernels for 0% -> 0%
where the time goes in v1:
time: 32.4 us; the launch traced here: 32.3 us
  Pallas kernels  31.6 us (98%)
  between operations  0.64 us (2%)
    pallas_call x1, Pallas kernels, per_device(): pl.pallas_call(kernel, out_shape=(jax.ShapeDtypeStruct((rows, SUB, width)...  26.6 us
    pallas_call x1, Pallas kernels, per_device(): pl.pallas_call(store, out_shape=(jax.ShapeDtypeStruct(previous.shape, f32...  5.01 us

profile of v1, /device:TPU:128, one launch (start us, length us, event | category | flops | bytes accessed | tf_op | source)
XLA Modules:
  0.0 32.3 jit_solution(1975490837420245078)
XLA Ops:
  0.6 26.6 %relax.1 = (f32[16,8,512]{2,1,0:T(8,128)}, f32[16,16,8,512]{3,2,1,0:T(8,128)}, f32[1,128]{1,0:T(1,128)}) custom-call(f32[16,4096]{1,0:T(8,128)} %refs_0_.1, f32[2,16,4096]{2,1,0:T(8,128)} %refs_1_.1, s32[16,4096]{1,0:T(8,128)} %refs_2_.1, s32[16,4096]{1,0:T(8,128)} %refs_3_.1, f32[16]{0:T(128)} %refs_4_.1, f32[16,16,4096]{2,1,0:T(8,128)} %refs_5_.1), custom_call_target="tpu_custom_call" | custom-call | tf_op jit(solution)/shard_map/relax/pallas_call | solution.py:462
  27.3 5.0 %store.1 = (f32[16,16,4096]{2,1,0:T(8,128)}, f32[16,4096]{1,0:T(8,128)}, f32[16]{0:T(128)}) custom-call(f32[16,16,8,512]{3,2,1,0:T(8,128)} %get-tuple-element.9.refs_0_, f32[16,8,512]{2,1,0:T(8,128)} %get-tuple-element.10.refs_1_, f32[1,128]{1,0:T(1,128)} %get-tuple-element.11.refs_2_), custom_call_target="tpu_custom_call" | custom-call | tf_op jit(solution)/shard_map/store/pallas_call | solution.py:501

commit v2 on v1

--- a/solution.py
+++ b/solution.py
@@ -493,7 +493,10 @@
                 collective_id=0, has_side_effects=True, vmem_limit_bytes=VMEM_LIMIT
             ),
             name="relax",
-        )(surface, velocity, block_map, free_flags, block_rates, previous)
+        )(*(
+            pltpu.with_memory_space_constraint(value, pltpu.HBM)
+            for value in (surface, velocity, block_map, free_flags, block_rates, previous)
+        ))
 
         def store(*refs):
             store_kernel(rows, width, *refs)
@@ -508,6 +511,7 @@
             in_specs=[inside, inside, inside],
             out_specs=(hbm, hbm, inside),
             scratch_shapes=[dma((2 * SUB,))],
+            compiler_params=pltpu.CompilerParams(vmem_limit_bytes=1024 * 1024),
             name="store",
         )(field, new_surface, norm)
         return new_surface, field, norm
@@ -524,4 +528,4 @@
     )
 
 
-VMEM_LIMIT = 58 * 1024 * 1024
+VMEM_LIMIT = 40 * 1024 * 1024

time: 32.4 us -> 28 us (0.86)
  Pallas kernels: 31.6 us -> 27.3 us
    pallas_call x1, Pallas kernels: 5.01 us -> 2.73 us  [per_device(): pl.pallas_call(store, out_shape=(jax.ShapeDtypeStruct(previous.shape, f32...]
    pallas_call x1, Pallas kernels: 26.6 us -> 24.6 us  [per_device(): pl.pallas_call(kernel, out_shape=(jax.ShapeDtypeStruct((rows, SUB, width)...]
where the time goes in v2:
time: 28 us; the launch traced here: 27.9 us
  Pallas kernels  27.3 us (98%)
  between operations  0.64 us (2%)
    pallas_call x1, Pallas kernels, per_device(): pl.pallas_call(kernel, out_shape=(jax.ShapeDtypeStruct((rows, SUB, width)...  24.6 us
    pallas_call x1, Pallas kernels, per_device(): pl.pallas_call(store, out_shape=(jax.ShapeDtypeStruct(previous.shape, f32...  2.73 us

profile of v2, /device:TPU:128, one launch (start us, length us, event | category | flops | bytes accessed | tf_op | source)
XLA Modules:
  0.0 27.9 jit_solution(7122020577414315431)
XLA Ops:
  0.6 24.6 %relax.1 = (f32[16,8,512]{2,1,0:T(8,128)S(1)}, f32[16,16,8,512]{3,2,1,0:T(8,128)S(1)}, f32[1,128]{1,0:T(1,128)S(1)}) custom-call(f32[16,4096]{1,0:T(8,128)} %refs_0_.1, f32[2,16,4096]{2,1,0:T(8,128)} %refs_1_.1, s32[16,4096]{1,0:T(8,128)} %refs_2_.1, s32[16,4096]{1,0:T(8,128)} %refs_3_.1, f32[16]{0:T(128)} %refs_4_.1, f32[16,16,4096]{2,1,0:T(8,128)} %refs_5_.1), custom_call_target="tpu_custom_call" | custom-call | tf_op jit(solution)/shard_map/relax/pallas_call | solution.py:462
  25.2 2.7 %store.1 = (f32[16,16,4096]{2,1,0:T(8,128)}, f32[16,4096]{1,0:T(8,128)}, f32[16]{0:T(128)}) custom-call(f32[16,16,8,512]{3,2,1,0:T(8,128)S(1)} %get-tuple-element.9.refs_0_, f32[16,8,512]{2,1,0:T(8,128)S(1)} %get-tuple-element.10.refs_1_, f32[1,128]{1,0:T(1,128)S(1)} %get-tuple-element.11.refs_2_), custom_call_target="tpu_custom_call" | custom-call | tf_op jit(solution)/shard_map/store/pallas_call | solution.py:504

commit v3 on v2

--- a/solution.py
+++ b/solution.py
@@ -47,7 +47,7 @@
     prev, once, above, below, surf, vel, bmap, flags, rates,
     shift, wide, widest, squares, totals,
     load_sem, up_send, up_recv, down_send, down_recv, side_send, side_recv,
-    corner_send, corner_recv, sum_send, sum_recv,
+    corner_send, corner_recv, sum_send, sum_recv, relay_sem,
 ):
     lat = lax.axis_index("lat")
     depth = lax.axis_index("depth")
@@ -57,10 +57,8 @@
     up, down = {"depth": depth - 1}, {"depth": depth + 1}
 
     barrier = pltpu.get_barrier_semaphore()
-    for k in (1, n_depth - 1):
-        pl.semaphore_signal(
-            barrier, inc=1, device_id={"depth": lax.rem(depth + k, n_depth)}, device_id_type=MESH)
-    for have, target in ((has_left, left), (has_right, right)):
+    around = ((has_up, up), (has_down, down), (has_left, left), (has_right, right))
+    for have, target in around:
         @pl.when(have)
         def _():
             pl.semaphore_signal(barrier, inc=1, device_id=target, device_id_type=MESH)
@@ -125,7 +123,7 @@
             clear(below.at[at])
             clear(once.at[at])
 
-    pl.semaphore_wait(barrier, 2 + has_left.astype(jnp.int32) + has_right.astype(jnp.int32))
+    pl.semaphore_wait(barrier, sum(have.astype(jnp.int32) for have, _ in around))
 
     def remote(src, dst, send, recv, target):
         return pltpu.make_async_remote_copy(
@@ -154,17 +152,20 @@
         for copy in to_up:
             copy.start()
 
-    def sides(mine3, theirs3, mine2, theirs2, row, target):
+    def sides(mine3, theirs3, mine2, theirs2, near, far, row, target):
         return [
             remote(surf.at[mine3], surf.at[theirs3], side_send.at[row, 0], side_recv.at[row, 0], target),
             remote(vel.at[:, mine2], vel.at[:, theirs2], side_send.at[row, 1], side_recv.at[row, 1], target),
             remote(bmap.at[mine2], bmap.at[theirs2], side_send.at[row, 2], side_recv.at[row, 2], target),
             remote(flags.at[mine2], flags.at[theirs2], side_send.at[row, 3], side_recv.at[row, 3], target),
-            remote(prev.at[mine2], prev.at[theirs2], side_send.at[row, 4], side_recv.at[row, 4], target),
+            remote(prev.at[near[0]], prev.at[near[1]], side_send.at[row, 4], side_recv.at[row, 4], target),
+            remote(prev.at[far[0]], prev.at[far[1]], side_send.at[row, 5], side_recv.at[row, 5], target),
         ]
 
-    to_right = sides(slice(rows, rows + 3), slice(0, 3), slice(rows, rows + 2), slice(0, 2), 0, right)
-    to_left = sides(slice(3, 6), slice(rows + 3, rows + 6), slice(2, 4), slice(rows + 2, rows + 4), 1, left)
+    to_right = sides(slice(rows, rows + 3), slice(0, 3), slice(rows, rows + 2), slice(0, 2),
+                     (rows + 1, 1), (rows, 0), 0, right)
+    to_left = sides(slice(3, 6), slice(rows + 3, rows + 6), slice(2, 4), slice(rows + 2, rows + 4),
+                    (2, rows + 2), (3, rows + 3), 1, left)
 
     loaded("surface")
 
@@ -182,11 +183,13 @@
 
     @pl.when(has_right)
     def _():
-        to_right[4].start()
+        for copy in to_right[4:]:
+            copy.start()
 
     @pl.when(has_left)
     def _():
-        to_left[4].start()
+        for copy in to_left[4:]:
+            copy.start()
 
     lane, sub = iotas(width)
     masks = (lane == 0, sub == 0, lane == 127, sub == SUB - 1)
@@ -210,32 +213,6 @@
 
     lax.fori_loop(2, rows, sweep_once, 0)
 
-    @pl.when(has_left)
-    def _():
-        for copy in to_right[:4]:
-            copy.wait_recv()
-
-    @pl.when(has_right)
-    def _():
-        for copy in to_left[:4]:
-            copy.wait_recv()
-
-    corners = []
-    for number, (src, dst, lat_to, depth_to, have_to, lat_from, depth_from) in enumerate((
-        (prev.at[rows + 1, layers - 1], above.at[0, 1], lat + 1, depth + 1, (has_right, has_down), has_left, has_up),
-        (prev.at[2, layers - 1], above.at[rows + 1, 1], lat - 1, depth + 1, (has_left, has_down), has_right, has_up),
-        (prev.at[rows + 1, 0], below.at[0, 0], lat + 1, depth - 1, (has_right, has_up), has_left, has_down),
-        (prev.at[2, 0], below.at[rows + 1, 0], lat - 1, depth - 1, (has_left, has_up), has_right, has_down),
-    )):
-        copy = remote(src, dst, corner_send.at[number], corner_recv.at[number], {"lat": lat_to, "depth": depth_to})
-        goes = jnp.logical_and(*have_to)
-        comes = jnp.logical_and(lat_from, depth_from)
-        corners.append((copy, goes, comes))
-
-        @pl.when(goes)
-        def _():
-            copy.start()
-
     rate = [rates[k] for k in range(16)]
 
     def lookup(index):
@@ -257,37 +234,9 @@
             new_surface[i - 2] = new
         shift[i] = new - middle
 
-    def advect_inner(i, carry):
-        advect(i, True)
-        return carry
-
-    lax.fori_loop(2, rows + 2, advect_inner, 0)
-    for i in (0, 1, rows + 2, rows + 3):
-        advect(i, False)
-
     def widen(src, dst, i):
         here = src[i + 1]
         dst[i] = (CENTRE + 2.0) * here + (src[i] + src[i + 2]) + neighbours(here)
-
-    def widen_once(i, carry):
-        widen(shift, wide, i)
-        return carry
-
-    def widen_twice(i, carry):
-        widen(wide, widest, i)
-        return carry
-
-    lax.fori_loop(0, rows + 2, widen_once, 0)
-
-    @pl.when(jnp.logical_not(has_left))
-    def _():
-        clear(wide.at[0])
-
-    @pl.when(jnp.logical_not(has_right))
-    def _():
-        clear(wide.at[rows + 1])
-
-    lax.fori_loop(0, rows, widen_twice, 0)
 
     all_layers = layers * n_depth
     profile = [
@@ -329,61 +278,156 @@
         squares[i] = narrow(acc)
         return carry
 
-    lax.fori_loop(2, rows - 2, sweep_twice, 0)
+    def grouped(first, last, size, what):
+        def some(g, carry):
+            for k in range(size):
+                what(first + g * size + k)
+            return carry
+
+        count = (last - first) // size
+        if count:
+            lax.fori_loop(0, count, some, 0)
+        for i in range(first + count * size, last):
+            what(i)
+
+    grouped(3, rows + 1, 5, lambda i: advect(i, True))
+    grouped(3, rows - 1, 5, lambda i: widen(shift, wide, i))
+    grouped(3, rows - 3, 5, lambda i: widen(wide, widest, i))
+    lax.fori_loop(3, rows - 3, sweep_twice, 0)
 
     @pl.when(has_left)
     def _():
+        for copy in to_right[:4]:
+            copy.wait_recv()
+
+    @pl.when(has_right)
+    def _():
+        for copy in to_left[:4]:
+            copy.wait_recv()
+
+    corners = []
+    for number, (src, dst, lat_to, depth_to, have_to, lat_from, depth_from) in enumerate((
+        (prev.at[rows + 1, layers - 1], above.at[0, 1], lat + 1, depth + 1, (has_right, has_down), has_left, has_up),
+        (prev.at[2, layers - 1], above.at[rows + 1, 1], lat - 1, depth + 1, (has_left, has_down), has_right, has_up),
+        (prev.at[rows + 1, 0], below.at[0, 0], lat + 1, depth - 1, (has_right, has_up), has_left, has_down),
+        (prev.at[2, 0], below.at[rows + 1, 0], lat - 1, depth - 1, (has_left, has_up), has_right, has_down),
+    )):
+        copy = remote(src, dst, corner_send.at[number], corner_recv.at[number], {"lat": lat_to, "depth": depth_to})
+        goes = jnp.logical_and(*have_to)
+        comes = jnp.logical_and(lat_from, depth_from)
+        corners.append((copy, goes, comes))
+
+        @pl.when(goes)
+        def _():
+            copy.start()
+
+    for i in (0, 1, rows + 2, rows + 3):
+        advect(i, False)
+    for i in (2, rows + 1):
+        advect(i, True)
+    for i in (0, 1, 2, rows - 1, rows, rows + 1):
+        widen(shift, wide, i)
+
+    @pl.when(jnp.logical_not(has_left))
+    def _():
+        clear(wide.at[0])
+
+    @pl.when(jnp.logical_not(has_right))
+    def _():
+        clear(wide.at[rows + 1])
+
+    for i in (0, 1, 2, rows - 3, rows - 2, rows - 1):
+        widen(wide, widest, i)
+
+    @pl.when(has_left)
+    def _():
         to_right[4].wait_recv()
+
+    @pl.when(has_right)
+    def _():
+        to_left[4].wait_recv()
+
+    def one_each_side(k, carry):
+        sweep_once(1 + k * (rows - 1), 0)
+        return carry
+
+    def second_rows(k, carry):
+        sweep_twice(lax.select(k < 2, k + 1, rows - 5 + k), 0)
+        return carry
+
+    lax.fori_loop(0, 2, one_each_side, 0)
+    lax.fori_loop(0, 4, second_rows, 0)
+
+    def finish(first, last):
+        parts, values = {}, []
+        for i in range(first, last):
+            acc = None
+            for ref, near, far, outer, inner in ((above, 1, 0, 0, 1), (below, 0, 1, layers - 1, layers - 2)):
+                here = ref[i + 1, near]
+                around = ref[i, near] + ref[i + 2, near] + neighbours(here)
+                edge = mesh_out[i, outer] + SCALE * (2.0 * CENTRE * here + 2.0 * around + ref[i + 1, far])
+                next_in = mesh_out[i, inner] + SCALE * here
+                values += [(i, outer, edge), (i, inner, next_in)]
+                both = edge * edge + next_in * next_in
+                acc = both if acc is None else acc + both
+            parts[i] = squares[i] + narrow(acc)
+        for i, z, value in values:
+            mesh_out[i, z] = value
+        for i, value in parts.items():
+            squares[i] = value
+
+    def arrived(chunk):
+        @pl.when(has_up)
+        def _():
+            to_down[chunk].wait_recv()
+
+        @pl.when(has_down)
+        def _():
+            to_up[chunk].wait_recv()
+
+    early = 3 * CHUNKS // 4
+    for c in range(early):
+        arrived(c)
+
+    for have, target in ((has_up, up), (has_down, down)):
+        @pl.when(have)
+        def _():
+            pl.semaphore_signal(relay_sem, inc=1, device_id=target, device_id_type=MESH)
+
+    middle = early * step - 1
+    for first in range(3, middle, 4):
+        finish(first, min(first + 4, middle))
+
+    @pl.when(has_left)
+    def _():
+        to_right[5].wait_recv()
         sweep_once(0, 0)
 
     @pl.when(has_right)
     def _():
-        to_left[4].wait_recv()
+        to_left[5].wait_recv()
         sweep_once(rows + 1, 0)
 
-    sweep_once(1, 0)
-    sweep_once(rows, 0)
-
-    def at_edges(k, carry):
-        sweep_twice(k, 0)
-        sweep_twice(rows - 1 - k, 0)
+    def edge_rows(k, carry):
+        sweep_twice(k * (rows - 1), 0)
         return carry
 
-    lax.fori_loop(0, 2, at_edges, 0)
-
-    def finish(i, carry):
-        acc = None
-        for ref, near, far, outer, inner in ((above, 1, 0, 0, 1), (below, 0, 1, layers - 1, layers - 2)):
-            here = ref[i + 1, near]
-            around = ref[i, near] + ref[i + 2, near] + neighbours(here)
-            edge = mesh_out[i, outer] + SCALE * (2.0 * CENTRE * here + 2.0 * around + ref[i + 1, far])
-            next_in = mesh_out[i, inner] + SCALE * here
-            mesh_out[i, outer] = edge
-            mesh_out[i, inner] = next_in
-            both = edge * edge + next_in * next_in
-            acc = both if acc is None else acc + both
-        squares[i] = squares[i] + narrow(acc)
-        return carry
+    lax.fori_loop(0, 2, edge_rows, 0)
 
     for copy, goes, comes in corners:
         @pl.when(comes)
         def _():
             copy.wait_recv()
 
-    done = 0
-    for c in range(CHUNKS):
-        @pl.when(has_up)
-        def _():
-            to_down[c].wait_recv()
-
-        @pl.when(has_down)
-        def _():
-            to_up[c].wait_recv()
-
+    finish(0, 3)
+    done = middle
+    for c in range(early, CHUNKS):
+        arrived(c)
         ready = rows if c == CHUNKS - 1 else (c + 1) * step - 1
-        lax.fori_loop(done, ready, finish, 0)
+        finish(done, ready)
         done = ready
 
+    pl.semaphore_wait(relay_sem, has_up.astype(jnp.int32) + has_down.astype(jnp.int32))
     totals[depth] = jnp.sum(squares[...], axis=1)
     spread = []
     for k in range(1, n_depth):
@@ -429,7 +473,7 @@
         copy.wait_send()
 
 
-def store_kernel(rows, width, mesh_in, surface_in, norm_in, mesh_out, surface_out, norm_out, sem):
+def store_kernel(rows, width, mesh_in, surface_in, norm_in, mesh_out, surface_out, norm_out, norm, sem):
     copies = []
     for s in range(SUB):
         cols = slice(s * width, (s + 1) * width)
@@ -437,7 +481,10 @@
         copies.append(pltpu.make_async_copy(surface_in.at[:, s, :], surface_out.at[:, cols], sem.at[SUB + s]))
     for copy in copies:
         copy.start()
-    norm_out[...] = norm_in[0, :rows]
+    norm[...] = norm_in[0, :rows]
+    last = pltpu.make_async_copy(norm, norm_out, sem.at[2 * SUB])
+    last.start()
+    copies.append(last)
     for copy in copies:
         copy.wait()
 
@@ -485,9 +532,10 @@
                 vmem(n_depth, rows, 128),
                 dma((8 * SUB + 1,)),
                 dma((CHUNKS,)), dma((CHUNKS,)), dma((CHUNKS,)), dma((CHUNKS,)),
-                dma((2, 5)), dma((2, 5)),
+                dma((2, 6)), dma((2, 6)),
                 dma((4,)), dma((4,)),
                 dma((n_depth - 1,)), dma((n_depth - 1,)),
+                pltpu.SemaphoreType.REGULAR,
             ],
             compiler_params=pltpu.CompilerParams(
                 collective_id=0, has_side_effects=True, vmem_limit_bytes=VMEM_LIMIT
@@ -509,8 +557,8 @@
                 jax.ShapeDtypeStruct((rows,), f32),
             ),
             in_specs=[inside, inside, inside],
-            out_specs=(hbm, hbm, inside),
-            scratch_shapes=[dma((2 * SUB,))],
+            out_specs=(hbm, hbm, hbm),
+            scratch_shapes=[vmem(rows), dma((2 * SUB + 1,))],
             compiler_params=pltpu.CompilerParams(vmem_limit_bytes=1024 * 1024),
             name="store",
         )(field, new_surface, norm)

time: 28 us -> 25.9 us (0.925)
  the two profiles are of different devices: /device:TPU:128 before, /device:TPU:102 now
where the time goes in v3:
time: 25.9 us; the launch traced here: 25.8 us
  Pallas kernels  25.2 us (97%)
  between operations  0.64 us (2%)
    pallas_call x1, Pallas kernels, per_device(): pl.pallas_call(kernel, out_shape=(jax.ShapeDtypeStruct((rows, SUB, width)...  22.9 us
    pallas_call x1, Pallas kernels, per_device(): pl.pallas_call(store, out_shape=(jax.ShapeDtypeStruct(previous.shape, f32...  2.23 us

profile of v3, /device:TPU:102, one launch (start us, length us, event | category | flops | bytes accessed | tf_op | source)
XLA Modules:
  0.0 25.8 jit_solution(3310925451581884908)
XLA Ops:
  0.6 22.9 %relax.1 = (f32[16,8,512]{2,1,0:T(8,128)S(1)}, f32[16,16,8,512]{3,2,1,0:T(8,128)S(1)}, f32[1,128]{1,0:T(1,128)S(1)}) custom-call(f32[16,4096]{1,0:T(8,128)} %refs_0_.1, f32[2,16,4096]{2,1,0:T(8,128)} %refs_1_.1, s32[16,4096]{1,0:T(8,128)} %refs_2_.1, s32[16,4096]{1,0:T(8,128)} %refs_3_.1, f32[16]{0:T(128)} %refs_4_.1, f32[16,16,4096]{2,1,0:T(8,128)} %refs_5_.1), custom_call_target="tpu_custom_call" | custom-call | tf_op jit(solution)/shard_map/relax/pallas_call | solution.py:509
  23.6 2.2 %store.1 = (f32[16,16,4096]{2,1,0:T(8,128)}, f32[16,4096]{1,0:T(8,128)}, f32[16]{0:T(128)}) custom-call(f32[16,16,8,512]{3,2,1,0:T(8,128)S(1)} %get-tuple-element.9.refs_0_, f32[16,8,512]{2,1,0:T(8,128)S(1)} %get-tuple-element.10.refs_1_, f32[1,128]{1,0:T(1,128)S(1)} %get-tuple-element.11.refs_2_), custom_call_target="tpu_custom_call" | custom-call | tf_op jit(solution)/shard_map/store/pallas_call | solution.py:552

commit v4 on v3

--- a/solution.py
+++ b/solution.py
@@ -13,7 +13,6 @@
 CENTRE = KEEP / SHARE
 SCALE = SHARE * SHARE
 SUB = 8
-CHUNKS = 8
 
 
 def iotas(width):
@@ -43,9 +42,9 @@
 def relax_kernel(
     rows, layers, width, n_lat, n_depth,
     surface, velocity, block_map, free_flags, block_rates, previous,
-    new_surface, mesh_out, norm_out,
+    new_surface, mesh_out, totals,
     prev, once, above, below, surf, vel, bmap, flags, rates,
-    shift, wide, widest, squares, totals,
+    shift, wide, widest, squares,
     load_sem, up_send, up_recv, down_send, down_recv, side_send, side_recv,
     corner_send, corner_recv, sum_send, sum_recv, relay_sem,
 ):
@@ -79,6 +78,9 @@
     def loaded(name):
         for copy in groups[name]:
             copy.wait()
+
+    pieces = [(0, 1), (rows - 1, rows)] + [(r, r + 2) for r in range(1, rows - 3, 2)]
+    pieces += [(rows - 3, rows - 2), (rows - 2, rows - 1)]
 
     cols = [slice(s * width, (s + 1) * width) for s in range(SUB)]
     own = slice(2, 2 + rows)
@@ -131,12 +133,10 @@
             device_id=target, device_id_type=MESH,
         )
 
-    step = rows // CHUNKS
     last_two, first_two = slice(layers - 2, layers), slice(0, 2)
     to_down, to_up = [], []
-    for c in range(CHUNKS):
-        mine = slice(2 + c * step, 2 + (c + 1) * step)
-        theirs = slice(1 + c * step, 1 + (c + 1) * step)
+    for c, (first, last) in enumerate(pieces):
+        mine, theirs = slice(2 + first, 2 + last), slice(1 + first, 1 + last)
         to_down.append(remote(prev.at[mine, last_two], above.at[theirs], down_send.at[c], down_recv.at[c], down))
         to_up.append(remote(prev.at[mine, first_two], below.at[theirs], up_send.at[c], up_recv.at[c], up))
 
@@ -278,6 +278,33 @@
         squares[i] = narrow(acc)
         return carry
 
+    def arrived(chunk):
+        @pl.when(has_up)
+        def _():
+            to_down[chunk].wait_recv()
+
+        @pl.when(has_down)
+        def _():
+            to_up[chunk].wait_recv()
+
+    arrived(0)
+    arrived(1)
+    corners = []
+    for number, (ref, near, depth_from) in enumerate(((above, 1, has_up), (below, 0, has_down))):
+        for side, (src, dst, goes, comes, target) in enumerate((
+            (rows, 0, has_right, has_left, right),
+            (1, rows + 1, has_left, has_right, left),
+        )):
+            copy = remote(
+                ref.at[src, near], ref.at[dst, near],
+                corner_send.at[2 * number + side], corner_recv.at[2 * number + side], target)
+            goes, comes = jnp.logical_and(goes, depth_from), jnp.logical_and(comes, depth_from)
+            corners.append((copy, goes, comes))
+
+            @pl.when(goes)
+            def _():
+                copy.start()
+
     def grouped(first, last, size, what):
         def some(g, carry):
             for k in range(size):
@@ -304,22 +331,6 @@
     def _():
         for copy in to_left[:4]:
             copy.wait_recv()
-
-    corners = []
-    for number, (src, dst, lat_to, depth_to, have_to, lat_from, depth_from) in enumerate((
-        (prev.at[rows + 1, layers - 1], above.at[0, 1], lat + 1, depth + 1, (has_right, has_down), has_left, has_up),
-        (prev.at[2, layers - 1], above.at[rows + 1, 1], lat - 1, depth + 1, (has_left, has_down), has_right, has_up),
-        (prev.at[rows + 1, 0], below.at[0, 0], lat + 1, depth - 1, (has_right, has_up), has_left, has_down),
-        (prev.at[2, 0], below.at[rows + 1, 0], lat - 1, depth - 1, (has_left, has_up), has_right, has_down),
-    )):
-        copy = remote(src, dst, corner_send.at[number], corner_recv.at[number], {"lat": lat_to, "depth": depth_to})
-        goes = jnp.logical_and(*have_to)
-        comes = jnp.logical_and(lat_from, depth_from)
-        corners.append((copy, goes, comes))
-
-        @pl.when(goes)
-        def _():
-            copy.start()
 
     for i in (0, 1, rows + 2, rows + 3):
         advect(i, False)
@@ -376,17 +387,8 @@
         for i, value in parts.items():
             squares[i] = value
 
-    def arrived(chunk):
-        @pl.when(has_up)
-        def _():
-            to_down[chunk].wait_recv()
-
-        @pl.when(has_down)
-        def _():
-            to_up[chunk].wait_recv()
-
-    early = 3 * CHUNKS // 4
-    for c in range(early):
+    early = 7
+    for c in range(2, early):
         arrived(c)
 
     for have, target in ((has_up, up), (has_down, down)):
@@ -394,7 +396,7 @@
         def _():
             pl.semaphore_signal(relay_sem, inc=1, device_id=target, device_id_type=MESH)
 
-    middle = early * step - 1
+    middle = pieces[early - 1][1] - 1
     for first in range(3, middle, 4):
         finish(first, min(first + 4, middle))
 
@@ -421,9 +423,9 @@
 
     finish(0, 3)
     done = middle
-    for c in range(early, CHUNKS):
+    for c in range(early, len(pieces)):
         arrived(c)
-        ready = rows if c == CHUNKS - 1 else (c + 1) * step - 1
+        ready = rows if c == len(pieces) - 1 else pieces[c][1] - 1
         finish(done, ready)
         done = ready
 
@@ -437,12 +439,6 @@
         spread.append(copy)
     for copy in spread:
         copy.wait_recv()
-    total = totals[0]
-    for k in range(1, n_depth):
-        total = total + totals[k]
-    norm = jnp.sqrt(jnp.sum(total, axis=1, keepdims=True) / (all_layers * SUB * width))
-    spot = lax.broadcasted_iota(jnp.int32, (rows, 128), 0) == lax.broadcasted_iota(jnp.int32, (rows, 128), 1)
-    norm_out[...] = jnp.sum(jnp.where(spot, norm, 0.0), axis=0, keepdims=True)
 
     @pl.when(has_down)
     def _():
@@ -473,7 +469,7 @@
         copy.wait_send()
 
 
-def store_kernel(rows, width, mesh_in, surface_in, norm_in, mesh_out, surface_out, norm_out, norm, sem):
+def store_kernel(rows, width, mesh_in, surface_in, totals, mesh_out, surface_out, norm_out, norm, sem):
     copies = []
     for s in range(SUB):
         cols = slice(s * width, (s + 1) * width)
@@ -481,7 +477,13 @@
         copies.append(pltpu.make_async_copy(surface_in.at[:, s, :], surface_out.at[:, cols], sem.at[SUB + s]))
     for copy in copies:
         copy.start()
-    norm[...] = norm_in[0, :rows]
+    total = totals[0]
+    for k in range(1, totals.shape[0]):
+        total = total + totals[k]
+    nodes = mesh_in.shape[1] * totals.shape[0] * SUB * width
+    root = jnp.sqrt(jnp.sum(total, axis=1, keepdims=True) / nodes)
+    spot = lax.broadcasted_iota(jnp.int32, (rows, 128), 0) == lax.broadcasted_iota(jnp.int32, (rows, 128), 1)
+    norm[...] = jnp.sum(jnp.where(spot, root, 0.0), axis=0)[:rows]
     last = pltpu.make_async_copy(norm, norm_out, sem.at[2 * SUB])
     last.start()
     copies.append(last)
@@ -511,7 +513,7 @@
             out_shape=(
                 jax.ShapeDtypeStruct((rows, SUB, width), f32),
                 jax.ShapeDtypeStruct((rows, layers, SUB, width), f32),
-                jax.ShapeDtypeStruct((1, 128), f32),
+                jax.ShapeDtypeStruct((n_depth, rows, 128), f32),
             ),
             in_specs=[hbm] * 6,
             out_specs=(inside, inside, inside),
@@ -529,9 +531,8 @@
                 vmem(rows + 2, SUB, width),
                 vmem(rows, SUB, width),
                 vmem(rows, SUB, 128),
-                vmem(n_depth, rows, 128),
                 dma((8 * SUB + 1,)),
-                dma((CHUNKS,)), dma((CHUNKS,)), dma((CHUNKS,)), dma((CHUNKS,)),
+                dma((rows,)), dma((rows,)), dma((rows,)), dma((rows,)),
                 dma((2, 6)), dma((2, 6)),
                 dma((4,)), dma((4,)),
                 dma((n_depth - 1,)), dma((n_depth - 1,)),

time: 25.9 us -> 25.1 us (0.969)
  the two profiles are of different devices: /device:TPU:102 before, /device:TPU:128 now
where the time goes in v4:
time: 25.1 us; the launch traced here: 25 us
  Pallas kernels  24.3 us (97%)
  between operations  0.64 us (3%)
    pallas_call x1, Pallas kernels, per_device(): pl.pallas_call(kernel, out_shape=(jax.ShapeDtypeStruct((rows, SUB, width)...  22.1 us
    pallas_call x1, Pallas kernels, per_device(): pl.pallas_call(store, out_shape=(jax.ShapeDtypeStruct(previous.shape, f32...  2.23 us

profile of v4, /device:TPU:128, one launch (start us, length us, event | category | flops | bytes accessed | tf_op | source)
XLA Modules:
  0.0 25.0 jit_solution(3954809765947200423)
XLA Ops:
  0.6 22.1 %relax.1 = (f32[16,8,512]{2,1,0:T(8,128)S(1)}, f32[16,16,8,512]{3,2,1,0:T(8,128)S(1)}, f32[4,16,128]{2,1,0:T(8,128)S(1)}) custom-call(f32[16,4096]{1,0:T(8,128)} %refs_0_.1, f32[2,16,4096]{2,1,0:T(8,128)} %refs_1_.1, s32[16,4096]{1,0:T(8,128)} %refs_2_.1, s32[16,4096]{1,0:T(8,128)} %refs_3_.1, f32[16]{0:T(128)} %refs_4_.1, f32[16,16,4096]{2,1,0:T(8,128)} %refs_5_.1), custom_call_target="tpu_custom_call" | custom-call | tf_op jit(solution)/shard_map/relax/pallas_call | solution.py:511
  22.7 2.2 %store.1 = (f32[16,16,4096]{2,1,0:T(8,128)}, f32[16,4096]{1,0:T(8,128)}, f32[16]{0:T(128)}) custom-call(f32[16,16,8,512]{3,2,1,0:T(8,128)S(1)} %get-tuple-element.9.refs_0_, f32[16,8,512]{2,1,0:T(8,128)S(1)} %get-tuple-element.10.refs_1_, f32[4,16,128]{2,1,0:T(8,128)S(1)} %get-tuple-element.11.refs_2_), custom_call_target="tpu_custom_call" | custom-call | tf_op jit(solution)/shard_map/store/pallas_call | solution.py:553

commit v5 on v4

--- a/solution.py
+++ b/solution.py
@@ -45,8 +45,8 @@
     new_surface, mesh_out, totals,
     prev, once, above, below, surf, vel, bmap, flags, rates,
     shift, wide, widest, squares,
-    load_sem, up_send, up_recv, down_send, down_recv, side_send, side_recv,
-    corner_send, corner_recv, sum_send, sum_recv, relay_sem,
+    load_sem, z_send, up_recv, down_recv, side_send, side_recv,
+    corner_send, corner_recv, sum_sem, relay_sem,
 ):
     lat = lax.axis_index("lat")
     depth = lax.axis_index("depth")
@@ -62,42 +62,35 @@
         def _():
             pl.semaphore_signal(barrier, inc=1, device_id=target, device_id_type=MESH)
 
-    count = 0
-    groups = {}
-
-    def load(name, pairs):
-        nonlocal count
-        copies = []
+    def settled(ref, sem):
+        pltpu.make_async_copy(ref, ref, sem).wait()
+
+    def load(sem, pairs):
         for src, dst in pairs:
-            copy = pltpu.make_async_copy(src, dst, load_sem.at[count])
-            copy.start()
-            copies.append(copy)
-            count += 1
-        groups[name] = copies
-
-    def loaded(name):
-        for copy in groups[name]:
-            copy.wait()
-
-    pieces = [(0, 1), (rows - 1, rows)] + [(r, r + 2) for r in range(1, rows - 3, 2)]
-    pieces += [(rows - 3, rows - 2), (rows - 2, rows - 1)]
+            pltpu.make_async_copy(src, dst, sem).start()
+
+    pieces = [
+        (0, 1, 0), (rows - 1, rows, 0), (1, rows - 5, 1), (rows - 5, rows - 3, 2),
+        (rows - 3, rows - 2, 3), (rows - 2, rows - 1, 4),
+    ]
 
     cols = [slice(s * width, (s + 1) * width) for s in range(SUB)]
     own = slice(2, 2 + rows)
-    load("outer", [
+    load(load_sem.at[0], [
         (previous.at[:, part, cols[s]], prev.at[own, part, s, :])
         for part in (slice(layers - 2, layers), slice(0, 2)) for s in range(SUB)
     ])
-    load("surface",
+    load(load_sem.at[1],
          [(surface.at[:, cols[s]], surf.at[slice(3, 3 + rows), s, :]) for s in range(SUB)]
          + [(velocity.at[:, :, cols[s]], vel.at[:, own, s, :]) for s in range(SUB)]
          + [(block_map.at[:, cols[s]], bmap.at[own, s, :]) for s in range(SUB)]
-         + [(free_flags.at[:, cols[s]], flags.at[own, s, :]) for s in range(SUB)]
-         + [(block_rates, rates)])
-    load("inner", [
+         + [(free_flags.at[:, cols[s]], flags.at[own, s, :]) for s in range(SUB)])
+    load(load_sem.at[2], [
         (previous.at[:, part, cols[s]], prev.at[own, part, s, :])
         for part in (slice(2, SUB), slice(layers - SUB, layers - 2)) for s in range(SUB)
     ])
+    rates_copy = pltpu.make_async_copy(block_rates, rates, load_sem.at[3])
+    rates_copy.start()
 
     def clear(ref):
         ref[...] = jnp.zeros(ref.shape, ref.dtype)
@@ -135,12 +128,12 @@
 
     last_two, first_two = slice(layers - 2, layers), slice(0, 2)
     to_down, to_up = [], []
-    for c, (first, last) in enumerate(pieces):
+    for first, last, c in pieces:
         mine, theirs = slice(2 + first, 2 + last), slice(1 + first, 1 + last)
-        to_down.append(remote(prev.at[mine, last_two], above.at[theirs], down_send.at[c], down_recv.at[c], down))
-        to_up.append(remote(prev.at[mine, first_two], below.at[theirs], up_send.at[c], up_recv.at[c], up))
-
-    loaded("outer")
+        to_down.append(remote(prev.at[mine, last_two], above.at[theirs], z_send.at[0], down_recv.at[c], down))
+        to_up.append(remote(prev.at[mine, first_two], below.at[theirs], z_send.at[1], up_recv.at[c], up))
+
+    settled(prev.at[own, slice(0, 4)], load_sem.at[0])
 
     @pl.when(has_down)
     def _():
@@ -155,19 +148,22 @@
     def sides(mine3, theirs3, mine2, theirs2, near, far, row, target):
         return [
             remote(surf.at[mine3], surf.at[theirs3], side_send.at[row, 0], side_recv.at[row, 0], target),
-            remote(vel.at[:, mine2], vel.at[:, theirs2], side_send.at[row, 1], side_recv.at[row, 1], target),
-            remote(bmap.at[mine2], bmap.at[theirs2], side_send.at[row, 2], side_recv.at[row, 2], target),
-            remote(flags.at[mine2], flags.at[theirs2], side_send.at[row, 3], side_recv.at[row, 3], target),
-            remote(prev.at[near[0]], prev.at[near[1]], side_send.at[row, 4], side_recv.at[row, 4], target),
-            remote(prev.at[far[0]], prev.at[far[1]], side_send.at[row, 5], side_recv.at[row, 5], target),
+            remote(vel.at[:, mine2], vel.at[:, theirs2], side_send.at[row, 0], side_recv.at[row, 0], target),
+            remote(bmap.at[mine2], bmap.at[theirs2], side_send.at[row, 0], side_recv.at[row, 0], target),
+            remote(flags.at[mine2], flags.at[theirs2], side_send.at[row, 0], side_recv.at[row, 0], target),
+            remote(prev.at[near[0]], prev.at[near[1]], side_send.at[row, 1], side_recv.at[row, 1], target),
+            remote(prev.at[far[0]], prev.at[far[1]], side_send.at[row, 1], side_recv.at[row, 2], target),
         ]
+
+    edge_bytes = surf.at[slice(0, 3 + 4 * 2)]
 
     to_right = sides(slice(rows, rows + 3), slice(0, 3), slice(rows, rows + 2), slice(0, 2),
                      (rows + 1, 1), (rows, 0), 0, right)
     to_left = sides(slice(3, 6), slice(rows + 3, rows + 6), slice(2, 4), slice(rows + 2, rows + 4),
                     (2, rows + 2), (3, rows + 3), 1, left)
 
-    loaded("surface")
+    settled(prev.at[own, slice(0, 5)], load_sem.at[1])
+    rates_copy.wait()
 
     @pl.when(has_right)
     def _():
@@ -179,7 +175,7 @@
         for copy in to_left[:4]:
             copy.start()
 
-    loaded("inner")
+    settled(prev.at[own, slice(2, layers - 2)], load_sem.at[2])
 
     @pl.when(has_right)
     def _():
@@ -278,17 +274,18 @@
         squares[i] = narrow(acc)
         return carry
 
-    def arrived(chunk):
+    def arrived(c):
+        size = sum(last - first for first, last, sem in pieces if sem == c)
+
         @pl.when(has_up)
         def _():
-            to_down[chunk].wait_recv()
+            settled(above.at[slice(0, size)], down_recv.at[c])
 
         @pl.when(has_down)
         def _():
-            to_up[chunk].wait_recv()
+            settled(below.at[slice(0, size)], up_recv.at[c])
 
     arrived(0)
-    arrived(1)
     corners = []
     for number, (ref, near, depth_from) in enumerate(((above, 1, has_up), (below, 0, has_down))):
         for side, (src, dst, goes, comes, target) in enumerate((
@@ -324,13 +321,11 @@
 
     @pl.when(has_left)
     def _():
-        for copy in to_right[:4]:
-            copy.wait_recv()
+        settled(edge_bytes, side_recv.at[0, 0])
 
     @pl.when(has_right)
     def _():
-        for copy in to_left[:4]:
-            copy.wait_recv()
+        settled(edge_bytes, side_recv.at[1, 0])
 
     for i in (0, 1, rows + 2, rows + 3):
         advect(i, False)
@@ -387,16 +382,14 @@
         for i, value in parts.items():
             squares[i] = value
 
-    early = 7
-    for c in range(2, early):
-        arrived(c)
+    arrived(1)
 
     for have, target in ((has_up, up), (has_down, down)):
         @pl.when(have)
         def _():
             pl.semaphore_signal(relay_sem, inc=1, device_id=target, device_id_type=MESH)
 
-    middle = pieces[early - 1][1] - 1
+    middle = rows - 6
     for first in range(3, middle, 4):
         finish(first, min(first + 4, middle))
 
@@ -423,58 +416,45 @@
 
     finish(0, 3)
     done = middle
-    for c in range(early, len(pieces)):
+    for c, ready in ((2, rows - 4), (3, rows - 3), (4, rows)):
         arrived(c)
-        ready = rows if c == len(pieces) - 1 else pieces[c][1] - 1
         finish(done, ready)
         done = ready
 
     pl.semaphore_wait(relay_sem, has_up.astype(jnp.int32) + has_down.astype(jnp.int32))
     totals[depth] = jnp.sum(squares[...], axis=1)
-    spread = []
     for k in range(1, n_depth):
         target = lax.rem(depth + k, n_depth)
-        copy = remote(totals.at[depth], totals.at[depth], sum_send.at[k - 1], sum_recv.at[k - 1], {"depth": target})
+        copy = remote(totals.at[depth], totals.at[depth], sum_sem.at[0], sum_sem.at[1], {"depth": target})
         copy.start()
-        spread.append(copy)
-    for copy in spread:
-        copy.wait_recv()
-
-    @pl.when(has_down)
-    def _():
-        for copy in to_down:
-            copy.wait_send()
-
-    @pl.when(has_up)
-    def _():
-        for copy in to_up:
-            copy.wait_send()
-
-    @pl.when(has_right)
-    def _():
-        for copy in to_right:
-            copy.wait_send()
-
-    @pl.when(has_left)
-    def _():
-        for copy in to_left:
-            copy.wait_send()
+    everyone_else = totals.at[slice(0, n_depth - 1)]
+    settled(everyone_else, sum_sem.at[1])
+
+    for have, sem in ((has_down, z_send.at[0]), (has_up, z_send.at[1])):
+        @pl.when(have)
+        def _():
+            settled(prev.at[own, slice(0, 2)], sem)
+
+    for have, row in ((has_right, 0), (has_left, 1)):
+        @pl.when(have)
+        def _():
+            settled(edge_bytes, side_send.at[row, 0])
+            settled(prev.at[slice(0, 2)], side_send.at[row, 1])
 
     for copy, goes, comes in corners:
         @pl.when(goes)
         def _():
             copy.wait_send()
 
-    for copy in spread:
-        copy.wait_send()
+    settled(everyone_else, sum_sem.at[0])
 
 
 def store_kernel(rows, width, mesh_in, surface_in, totals, mesh_out, surface_out, norm_out, norm, sem):
     copies = []
     for s in range(SUB):
         cols = slice(s * width, (s + 1) * width)
-        copies.append(pltpu.make_async_copy(mesh_in.at[:, :, s, :], mesh_out.at[:, :, cols], sem.at[s]))
-        copies.append(pltpu.make_async_copy(surface_in.at[:, s, :], surface_out.at[:, cols], sem.at[SUB + s]))
+        copies.append(pltpu.make_async_copy(mesh_in.at[:, :, s, :], mesh_out.at[:, :, cols], sem.at[0]))
+        copies.append(pltpu.make_async_copy(surface_in.at[:, s, :], surface_out.at[:, cols], sem.at[1]))
     for copy in copies:
         copy.start()
     total = totals[0]
@@ -484,11 +464,11 @@
     root = jnp.sqrt(jnp.sum(total, axis=1, keepdims=True) / nodes)
     spot = lax.broadcasted_iota(jnp.int32, (rows, 128), 0) == lax.broadcasted_iota(jnp.int32, (rows, 128), 1)
     norm[...] = jnp.sum(jnp.where(spot, root, 0.0), axis=0)[:rows]
-    last = pltpu.make_async_copy(norm, norm_out, sem.at[2 * SUB])
+    last = pltpu.make_async_copy(norm, norm_out, sem.at[2])
     last.start()
-    copies.append(last)
-    for copy in copies:
-        copy.wait()
+    last.wait()
+    for ref, k in ((mesh_in, 0), (surface_in, 1)):
+        pltpu.make_async_copy(ref, ref, sem.at[k]).wait()
 
 
 def solution(mesh):
@@ -531,11 +511,11 @@
                 vmem(rows + 2, SUB, width),
                 vmem(rows, SUB, width),
                 vmem(rows, SUB, 128),
-                dma((8 * SUB + 1,)),
-                dma((rows,)), dma((rows,)), dma((rows,)), dma((rows,)),
-                dma((2, 6)), dma((2, 6)),
+                dma((4,)),
+                dma((2,)), dma((5,)), dma((5,)),
+                dma((2, 2)), dma((2, 3)),
                 dma((4,)), dma((4,)),
-                dma((n_depth - 1,)), dma((n_depth - 1,)),
+                dma((2,)),
                 pltpu.SemaphoreType.REGULAR,
             ],
             compiler_params=pltpu.CompilerParams(
@@ -559,7 +539,7 @@
             ),
             in_specs=[inside, inside, inside],
             out_specs=(hbm, hbm, hbm),
-            scratch_shapes=[vmem(rows), dma((2 * SUB + 1,))],
+            scratch_shapes=[vmem(rows), dma((3,))],
             compiler_params=pltpu.CompilerParams(vmem_limit_bytes=1024 * 1024),
             name="store",
         )(field, new_surface, norm)

time: 25.1 us -> 23.7 us (0.944)
  Pallas kernels: 24.3 us -> 22.8 us
    pallas_call x1, Pallas kernels: 22.1 us -> 20.7 us  [per_device(): pl.pallas_call(kernel, out_shape=(jax.ShapeDtypeStruct((rows, SUB, width)...]
where the time goes in v5:
time: 23.7 us; the launch traced here: 23.4 us
  Pallas kernels  22.8 us (96%)
  between operations  0.64 us (3%)
    pallas_call x1, Pallas kernels, per_device(): pl.pallas_call(kernel, out_shape=(jax.ShapeDtypeStruct((rows, SUB, width)...  20.7 us
    pallas_call x1, Pallas kernels, per_device(): pl.pallas_call(store, out_shape=(jax.ShapeDtypeStruct(previous.shape, f32...  2.11 us

profile of v5, /device:TPU:128, one launch (start us, length us, event | category | flops | bytes accessed | tf_op | source)
XLA Modules:
  0.0 23.4 jit_solution(17465617659533829640)
XLA Ops:
  0.6 20.7 %relax.1 = (f32[16,8,512]{2,1,0:T(8,128)S(1)}, f32[16,16,8,512]{3,2,1,0:T(8,128)S(1)}, f32[4,16,128]{2,1,0:T(8,128)S(1)}) custom-call(f32[16,4096]{1,0:T(8,128)} %refs_0_.1, f32[2,16,4096]{2,1,0:T(8,128)} %refs_1_.1, s32[16,4096]{1,0:T(8,128)} %refs_2_.1, s32[16,4096]{1,0:T(8,128)} %refs_3_.1, f32[16]{0:T(128)} %refs_4_.1, f32[16,16,4096]{2,1,0:T(8,128)} %refs_5_.1), custom_call_target="tpu_custom_call" | custom-call | tf_op jit(solution)/shard_map/relax/pallas_call | solution.py:491
  21.3 2.1 %store.1 = (f32[16,16,4096]{2,1,0:T(8,128)}, f32[16,4096]{1,0:T(8,128)}, f32[16]{0:T(128)}) custom-call(f32[16,16,8,512]{3,2,1,0:T(8,128)S(1)} %get-tuple-element.9.refs_0_, f32[16,8,512]{2,1,0:T(8,128)S(1)} %get-tuple-element.10.refs_1_, f32[4,16,128]{2,1,0:T(8,128)S(1)} %get-tuple-element.11.refs_2_), custom_call_target="tpu_custom_call" | custom-call | tf_op jit(solution)/shard_map/store/pallas_call | solution.py:533

commit v6 on v5

--- a/solution.py
+++ b/solution.py
@@ -13,6 +13,7 @@
 CENTRE = KEEP / SHARE
 SCALE = SHARE * SHARE
 SUB = 8
+FIRST = 9
 
 
 def iotas(width):
@@ -70,8 +71,8 @@
             pltpu.make_async_copy(src, dst, sem).start()
 
     pieces = [
-        (0, 1, 0), (rows - 1, rows, 0), (1, rows - 5, 1), (rows - 5, rows - 3, 2),
-        (rows - 3, rows - 2, 3), (rows - 2, rows - 1, 4),
+        (0, 1, 0), (rows - 1, rows, 0), (1, FIRST, 1), (FIRST, rows - 4, 2),
+        (rows - 4, rows - 2, 3), (rows - 2, rows - 1, 4),
     ]
 
     cols = [slice(s * width, (s + 1) * width) for s in range(SUB)]
@@ -135,15 +136,21 @@
 
     settled(prev.at[own, slice(0, 4)], load_sem.at[0])
 
-    @pl.when(has_down)
-    def _():
-        for copy in to_down:
-            copy.start()
-
-    @pl.when(has_up)
-    def _():
-        for copy in to_up:
-            copy.start()
+    def send_layers(turn, part):
+        @pl.when(jnp.logical_and(has_down, turn))
+        def _():
+            for copy in to_down[part]:
+                copy.start()
+
+        @pl.when(jnp.logical_and(has_up, turn))
+        def _():
+            for copy in to_up[part]:
+                copy.start()
+
+    odd = lax.rem(lat, 2) == 1
+    held = jnp.logical_and(odd, lat != n_lat // 2 - 1)
+    send_layers(True, slice(0, 3))
+    send_layers(jnp.logical_not(held), slice(3, None))
 
     def sides(mine3, theirs3, mine2, theirs2, near, far, row, target):
         return [
@@ -286,6 +293,12 @@
             settled(below.at[slice(0, size)], up_recv.at[c])
 
     arrived(0)
+
+    for have, target in ((has_up, up), (has_down, down)):
+        @pl.when(have)
+        def _():
+            pl.semaphore_signal(relay_sem, inc=1, device_id=target, device_id_type=MESH)
+
     corners = []
     for number, (ref, near, depth_from) in enumerate(((above, 1, has_up), (below, 0, has_down))):
         for side, (src, dst, goes, comes, target) in enumerate((
@@ -345,24 +358,48 @@
     for i in (0, 1, 2, rows - 3, rows - 2, rows - 1):
         widen(wide, widest, i)
 
-    @pl.when(has_left)
-    def _():
-        to_right[4].wait_recv()
-
-    @pl.when(has_right)
-    def _():
-        to_left[4].wait_recv()
-
-    def one_each_side(k, carry):
-        sweep_once(1 + k * (rows - 1), 0)
-        return carry
-
-    def second_rows(k, carry):
-        sweep_twice(lax.select(k < 2, k + 1, rows - 5 + k), 0)
-        return carry
-
-    lax.fori_loop(0, 2, one_each_side, 0)
-    lax.fori_loop(0, 4, second_rows, 0)
+    even = jnp.logical_not(odd)
+    far_side = jnp.logical_or(jnp.logical_and(odd, has_right), jnp.logical_and(even, has_left))
+
+    def side_rows(at_left, kind):
+        first = lax.select(at_left, 0, rows - 1)
+        inward = lax.select(at_left, 1, -1)
+
+        def wait():
+            @pl.when(at_left)
+            def _():
+                to_right[kind].wait_recv()
+
+            @pl.when(jnp.logical_not(at_left))
+            def _():
+                to_left[kind].wait_recv()
+
+        return first, inward, wait
+
+    def near_rows(at_left, have):
+        first, inward, wait = side_rows(at_left, 4)
+        pl.when(have)(wait)
+        sweep_once(first + 1, 0)
+
+        def body(k, carry):
+            return sweep_twice(first + k * inward, 0)
+
+        lax.fori_loop(1, 3, body, 0)
+
+    def edge_row(at_left, have):
+        first, inward, wait = side_rows(at_left, 5)
+
+        @pl.when(have)
+        def _():
+            wait()
+            sweep_once(first + 1 - inward, 0)
+
+        sweep_twice(first, 0)
+
+    near_rows(odd, True)
+    edge_row(odd, True)
+    near_rows(even, far_side)
+    send_layers(held, slice(3, None))
 
     def finish(first, last):
         parts, values = {}, []
@@ -382,32 +419,11 @@
         for i, value in parts.items():
             squares[i] = value
 
+    edge_row(even, far_side)
+
     arrived(1)
-
-    for have, target in ((has_up, up), (has_down, down)):
-        @pl.when(have)
-        def _():
-            pl.semaphore_signal(relay_sem, inc=1, device_id=target, device_id_type=MESH)
-
-    middle = rows - 6
-    for first in range(3, middle, 4):
-        finish(first, min(first + 4, middle))
-
-    @pl.when(has_left)
-    def _():
-        to_right[5].wait_recv()
-        sweep_once(0, 0)
-
-    @pl.when(has_right)
-    def _():
-        to_left[5].wait_recv()
-        sweep_once(rows + 1, 0)
-
-    def edge_rows(k, carry):
-        sweep_twice(k * (rows - 1), 0)
-        return carry
-
-    lax.fori_loop(0, 2, edge_rows, 0)
+    finish(3, 6)
+    finish(6, FIRST - 1)
 
     for copy, goes, comes in corners:
         @pl.when(comes)
@@ -415,15 +431,17 @@
             copy.wait_recv()
 
     finish(0, 3)
-    done = middle
-    for c, ready in ((2, rows - 4), (3, rows - 3), (4, rows)):
-        arrived(c)
-        finish(done, ready)
-        done = ready
+    arrived(2)
+    finish(FIRST - 1, rows - 5)
+
+    arrived(3)
+    finish(rows - 5, rows - 3)
+    arrived(4)
+    finish(rows - 3, rows)
 
     pl.semaphore_wait(relay_sem, has_up.astype(jnp.int32) + has_down.astype(jnp.int32))
     totals[depth] = jnp.sum(squares[...], axis=1)
-    for k in range(1, n_depth):
+    for k in sorted(range(1, n_depth), key=lambda k: abs(2 * k - n_depth)):
         target = lax.rem(depth + k, n_depth)
         copy = remote(totals.at[depth], totals.at[depth], sum_sem.at[0], sum_sem.at[1], {"depth": target})
         copy.start()

time: 23.7 us -> 23.2 us (0.979)
  Pallas kernels: 22.8 us -> 22.5 us
    pallas_call x1, Pallas kernels: 20.7 us -> 20.4 us  [per_device(): pl.pallas_call(kernel, out_shape=(jax.ShapeDtypeStruct((rows, SUB, width)...]
where the time goes in v6:
time: 23.2 us; the launch traced here: 23.1 us
  Pallas kernels  22.5 us (97%)
  between operations  0.64 us (3%)
    pallas_call x1, Pallas kernels, per_device(): pl.pallas_call(kernel, out_shape=(jax.ShapeDtypeStruct((rows, SUB, width)...  20.4 us
    pallas_call x1, Pallas kernels, per_device(): pl.pallas_call(store, out_shape=(jax.ShapeDtypeStruct(previous.shape, f32...  2.11 us

profile of v6, /device:TPU:128, one launch (start us, length us, event | category | flops | bytes accessed | tf_op | source)
XLA Modules:
  0.0 23.1 jit_solution(10328668684180447742)
XLA Ops:
  0.6 20.4 %relax.1 = (f32[16,8,512]{2,1,0:T(8,128)S(1)}, f32[16,16,8,512]{3,2,1,0:T(8,128)S(1)}, f32[4,16,128]{2,1,0:T(8,128)S(1)}) custom-call(f32[16,4096]{1,0:T(8,128)} %refs_0_.1, f32[2,16,4096]{2,1,0:T(8,128)} %refs_1_.1, s32[16,4096]{1,0:T(8,128)} %refs_2_.1, s32[16,4096]{1,0:T(8,128)} %refs_3_.1, f32[16]{0:T(128)} %refs_4_.1, f32[16,16,4096]{2,1,0:T(8,128)} %refs_5_.1), custom_call_target="tpu_custom_call" | custom-call | tf_op jit(solution)/shard_map/relax/pallas_call | solution.py:509
  21.0 2.1 %store.1 = (f32[16,16,4096]{2,1,0:T(8,128)}, f32[16,4096]{1,0:T(8,128)}, f32[16]{0:T(128)}) custom-call(f32[16,16,8,512]{3,2,1,0:T(8,128)S(1)} %get-tuple-element.9.refs_0_, f32[16,8,512]{2,1,0:T(8,128)S(1)} %get-tuple-element.10.refs_1_, f32[4,16,128]{2,1,0:T(8,128)S(1)} %get-tuple-element.11.refs_2_), custom_call_target="tpu_custom_call" | custom-call | tf_op jit(solution)/shard_map/store/pallas_call | solution.py:551

commit v7 on v6

--- a/solution.py
+++ b/solution.py
@@ -13,7 +13,7 @@
 CENTRE = KEEP / SHARE
 SCALE = SHARE * SHARE
 SUB = 8
-FIRST = 9
+FIRST = 10
 
 
 def iotas(width):
@@ -148,7 +148,9 @@
                 copy.start()
 
     odd = lax.rem(lat, 2) == 1
-    held = jnp.logical_and(odd, lat != n_lat // 2 - 1)
+    half = n_lat // 2
+    late = jnp.logical_or(lat == 1, lat == half - 1)
+    held = jnp.logical_and(odd, jnp.logical_not(late))
     send_layers(True, slice(0, 3))
     send_layers(jnp.logical_not(held), slice(3, None))
 
@@ -419,21 +421,23 @@
         for i, value in parts.items():
             squares[i] = value
 
+    def middle():
+        arrived(2)
+        finish(FIRST - 1, rows - 5)
+
+    arrived(1)
+    for first in range(1, FIRST - 1, 4):
+        finish(first, min(first + 4, FIRST - 1))
+    pl.when(even)(middle)
     edge_row(even, far_side)
-
-    arrived(1)
-    finish(3, 6)
-    finish(6, FIRST - 1)
 
     for copy, goes, comes in corners:
         @pl.when(comes)
         def _():
             copy.wait_recv()
 
-    finish(0, 3)
-    arrived(2)
-    finish(FIRST - 1, rows - 5)
-
+    finish(0, 1)
+    pl.when(odd)(middle)
     arrived(3)
     finish(rows - 5, rows - 3)
     arrived(4)

time: 23.2 us -> 23.2 us (level); the launches traced: 23.1 us -> 22.8 us
  Pallas kernels: 22.5 us -> 22.1 us
    pallas_call x1, Pallas kernels: 20.4 us -> 20 us  [per_device(): pl.pallas_call(kernel, out_shape=(jax.ShapeDtypeStruct((rows, SUB, width)...]
where the time goes in v7:
time: 23.2 us; the launch traced here: 22.8 us
  Pallas kernels  22.1 us (95%)
  between operations  0.64 us (3%)
    pallas_call x1, Pallas kernels, per_device(): pl.pallas_call(kernel, out_shape=(jax.ShapeDtypeStruct((rows, SUB, width)...  20 us
    pallas_call x1, Pallas kernels, per_device(): pl.pallas_call(store, out_shape=(jax.ShapeDtypeStruct(previous.shape, f32...  2.11 us

profile of v7, /device:TPU:128, one launch (start us, length us, event | category | flops | bytes accessed | tf_op | source)
XLA Modules:
  0.0 22.8 jit_solution(6072355103810415103)
XLA Ops:
  0.6 20.0 %relax.1 = (f32[16,8,512]{2,1,0:T(8,128)S(1)}, f32[16,16,8,512]{3,2,1,0:T(8,128)S(1)}, f32[4,16,128]{2,1,0:T(8,128)S(1)}) custom-call(f32[16,4096]{1,0:T(8,128)} %refs_0_.1, f32[2,16,4096]{2,1,0:T(8,128)} %refs_1_.1, s32[16,4096]{1,0:T(8,128)} %refs_2_.1, s32[16,4096]{1,0:T(8,128)} %refs_3_.1, f32[16]{0:T(128)} %refs_4_.1, f32[16,16,4096]{2,1,0:T(8,128)} %refs_5_.1), custom_call_target="tpu_custom_call" | custom-call | tf_op jit(solution)/shard_map/relax/pallas_call | solution.py:513
  20.7 2.1 %store.1 = (f32[16,16,4096]{2,1,0:T(8,128)}, f32[16,4096]{1,0:T(8,128)}, f32[16]{0:T(128)}) custom-call(f32[16,16,8,512]{3,2,1,0:T(8,128)S(1)} %get-tuple-element.9.refs_0_, f32[16,8,512]{2,1,0:T(8,128)S(1)} %get-tuple-element.10.refs_1_, f32[4,16,128]{2,1,0:T(8,128)S(1)} %get-tuple-element.11.refs_2_), custom_call_target="tpu_custom_call" | custom-call | tf_op jit(solution)/shard_map/store/pallas_call | solution.py:555

commit v8 on v7

--- a/solution.py
+++ b/solution.py
@@ -150,7 +150,7 @@
     odd = lax.rem(lat, 2) == 1
     half = n_lat // 2
     late = jnp.logical_or(lat == 1, lat == half - 1)
-    held = jnp.logical_and(odd, jnp.logical_not(late))
+    held = jnp.logical_or(jnp.logical_and(odd, jnp.logical_not(late)), lat == 0)
     send_layers(True, slice(0, 3))
     send_layers(jnp.logical_not(held), slice(3, None))
 

time: 23.2 us -> 22.9 us (0.987); the launches traced: 22.8 us -> 22.8 us
  no operation moved by 1% of the time
where the time goes in v8:
time: 22.9 us; the launch traced here: 22.8 us
  Pallas kernels  22.1 us (97%)
  between operations  0.64 us (3%)
    pallas_call x1, Pallas kernels, per_device(): pl.pallas_call(kernel, out_shape=(jax.ShapeDtypeStruct((rows, SUB, width)...  20 us
    pallas_call x1, Pallas kernels, per_device(): pl.pallas_call(store, out_shape=(jax.ShapeDtypeStruct(previous.shape, f32...  2.11 us

profile of v8, /device:TPU:128, one launch (start us, length us, event | category | flops | bytes accessed | tf_op | source)
XLA Modules:
  0.0 22.8 jit_solution(15416986345622515695)
XLA Ops:
  0.6 20.0 %relax.1 = (f32[16,8,512]{2,1,0:T(8,128)S(1)}, f32[16,16,8,512]{3,2,1,0:T(8,128)S(1)}, f32[4,16,128]{2,1,0:T(8,128)S(1)}) custom-call(f32[16,4096]{1,0:T(8,128)} %refs_0_.1, f32[2,16,4096]{2,1,0:T(8,128)} %refs_1_.1, s32[16,4096]{1,0:T(8,128)} %refs_2_.1, s32[16,4096]{1,0:T(8,128)} %refs_3_.1, f32[16]{0:T(128)} %refs_4_.1, f32[16,16,4096]{2,1,0:T(8,128)} %refs_5_.1), custom_call_target="tpu_custom_call" | custom-call | tf_op jit(solution)/shard_map/relax/pallas_call | solution.py:513
  20.7 2.1 %store.1 = (f32[16,16,4096]{2,1,0:T(8,128)}, f32[16,4096]{1,0:T(8,128)}, f32[16]{0:T(128)}) custom-call(f32[16,16,8,512]{3,2,1,0:T(8,128)S(1)} %get-tuple-element.9.refs_0_, f32[16,8,512]{2,1,0:T(8,128)S(1)} %get-tuple-element.10.refs_1_, f32[4,16,128]{2,1,0:T(8,128)S(1)} %get-tuple-element.11.refs_2_), custom_call_target="tpu_custom_call" | custom-call | tf_op jit(solution)/shard_map/store/pallas_call | solution.py:555

commit v9 on v8

--- a/solution.py
+++ b/solution.py
@@ -13,7 +13,7 @@
 CENTRE = KEEP / SHARE
 SCALE = SHARE * SHARE
 SUB = 8
-FIRST = 10
+FIRST = 9
 
 
 def iotas(width):
@@ -400,8 +400,8 @@
 
     near_rows(odd, True)
     edge_row(odd, True)
+    send_layers(held, slice(3, None))
     near_rows(even, far_side)
-    send_layers(held, slice(3, None))
 
     def finish(first, last):
         parts, values = {}, []

time: 22.9 us -> 22.9 us (level)
  no operation moved by 1% of the time
where the time goes in v9:
time: 22.9 us; the launch traced here: 22.8 us
  Pallas kernels  22.1 us (97%)
  between operations  0.64 us (3%)
    pallas_call x1, Pallas kernels, per_device(): pl.pallas_call(kernel, out_shape=(jax.ShapeDtypeStruct((rows, SUB, width)...  20 us
    pallas_call x1, Pallas kernels, per_device(): pl.pallas_call(store, out_shape=(jax.ShapeDtypeStruct(previous.shape, f32...  2.11 us

profile of v9, /device:TPU:128, one launch (start us, length us, event | category | flops | bytes accessed | tf_op | source)
XLA Modules:
  0.0 22.8 jit_solution(272604790189118143)
XLA Ops:
  0.6 20.0 %relax.1 = (f32[16,8,512]{2,1,0:T(8,128)S(1)}, f32[16,16,8,512]{3,2,1,0:T(8,128)S(1)}, f32[4,16,128]{2,1,0:T(8,128)S(1)}) custom-call(f32[16,4096]{1,0:T(8,128)} %refs_0_.1, f32[2,16,4096]{2,1,0:T(8,128)} %refs_1_.1, s32[16,4096]{1,0:T(8,128)} %refs_2_.1, s32[16,4096]{1,0:T(8,128)} %refs_3_.1, f32[16]{0:T(128)} %refs_4_.1, f32[16,16,4096]{2,1,0:T(8,128)} %refs_5_.1), custom_call_target="tpu_custom_call" | custom-call | tf_op jit(solution)/shard_map/relax/pallas_call | solution.py:513
  20.7 2.1 %store.1 = (f32[16,16,4096]{2,1,0:T(8,128)}, f32[16,4096]{1,0:T(8,128)}, f32[16]{0:T(128)}) custom-call(f32[16,16,8,512]{3,2,1,0:T(8,128)S(1)} %get-tuple-element.9.refs_0_, f32[16,8,512]{2,1,0:T(8,128)S(1)} %get-tuple-element.10.refs_1_, f32[4,16,128]{2,1,0:T(8,128)S(1)} %get-tuple-element.11.refs_2_), custom_call_target="tpu_custom_call" | custom-call | tf_op jit(solution)/shard_map/store/pallas_call | solution.py:555

commit v10 on v8

--- a/solution.py
+++ b/solution.py
@@ -400,8 +400,10 @@
 
     near_rows(odd, True)
     edge_row(odd, True)
+    turn = lax.rem(lat, 8) == 7
+    send_layers(jnp.logical_and(held, turn), slice(3, None))
     near_rows(even, far_side)
-    send_layers(held, slice(3, None))
+    send_layers(jnp.logical_and(held, jnp.logical_not(turn)), slice(3, None))
 
     def finish(first, last):
         parts, values = {}, []

time: 22.9 us -> 23.3 us (1.017)
  the two profiles are of different devices: /device:TPU:128 before, /device:TPU:6 now
where the time goes in v10:
time: 23.3 us; the launch traced here: 23.2 us
  Pallas kernels  22.5 us (97%)
  between operations  0.64 us (3%)
    pallas_call x1, Pallas kernels, per_device(): pl.pallas_call(kernel, out_shape=(jax.ShapeDtypeStruct((rows, SUB, width)...  20.4 us
    pallas_call x1, Pallas kernels, per_device(): pl.pallas_call(store, out_shape=(jax.ShapeDtypeStruct(previous.shape, f32...  2.11 us

profile of v10, /device:TPU:6, one launch (start us, length us, event | category | flops | bytes accessed | tf_op | source)
XLA Modules:
  0.0 23.2 jit_solution(14525226858115695263)
XLA Ops:
  0.6 20.4 %relax.1 = (f32[16,8,512]{2,1,0:T(8,128)S(1)}, f32[16,16,8,512]{3,2,1,0:T(8,128)S(1)}, f32[4,16,128]{2,1,0:T(8,128)S(1)}) custom-call(f32[16,4096]{1,0:T(8,128)} %refs_0_.1, f32[2,16,4096]{2,1,0:T(8,128)} %refs_1_.1, s32[16,4096]{1,0:T(8,128)} %refs_2_.1, s32[16,4096]{1,0:T(8,128)} %refs_3_.1, f32[16]{0:T(128)} %refs_4_.1, f32[16,16,4096]{2,1,0:T(8,128)} %refs_5_.1), custom_call_target="tpu_custom_call" | custom-call | tf_op jit(solution)/shard_map/relax/pallas_call | solution.py:515
  21.0 2.1 %store.1 = (f32[16,16,4096]{2,1,0:T(8,128)}, f32[16,4096]{1,0:T(8,128)}, f32[16]{0:T(128)}) custom-call(f32[16,16,8,512]{3,2,1,0:T(8,128)S(1)} %get-tuple-element.9.refs_0_, f32[16,8,512]{2,1,0:T(8,128)S(1)} %get-tuple-element.10.refs_1_, f32[4,16,128]{2,1,0:T(8,128)S(1)} %get-tuple-element.11.refs_2_), custom_call_target="tpu_custom_call" | custom-call | tf_op jit(solution)/shard_map/store/pallas_call | solution.py:557
